TPU v7x, 32 devices: a whole 2x2x4 slice. The times are simulated.
32 devices in a mesh: samp: 16 (over z, y, x), tgt: 2 (over core).
Axes of the slice: x: 2, y: 2, z: 4, core: 2. Of those that a mesh axis runs over, the one named last changes fastest.
Arguments:
- samples: bfloat16 [3072, 128], P('samp'), may hold values from -6 to 6
- omega: bfloat16 [128, 4096], replicated, may hold values from -0.5 to 0.5
- phase: float32 [4096], replicated, may hold values from -3.140625 to 3.140625
- right_side: float32 [4096, 512], P('samp', 'tgt'), may hold values from -6 to 6
Outputs:
- weights: float32 [4096, 512], P('samp', 'tgt')
All inputs are finite; a program needn't handle non-finite values.
Results may differ from a plain program's by a relative error of at most 0.011.
The roundings to bfloat16 on the way count: a program that leaves them out, or rounds other values in their place, can miss the bound.
Values may be sent and summed in bfloat16 or wider, within the bound.
A program may use at most 128 MiB of HBM per device.

v0:
```python
import functools

import jax
import jax.numpy as jnp
from jax import lax
from jax.experimental import pallas as pl
from jax.experimental.pallas import tpu as pltpu
from jax.sharding import PartitionSpec as P

ridge = 1.0
HI = lax.Precision.HIGHEST
F32 = jnp.float32
BF16 = jnp.bfloat16
BLOCK = 128
GROUP = 4
MESH = pl.DeviceIdType.MESH


def precise_dot(left_matrix, right_matrix):
    return jnp.dot(left_matrix, right_matrix, precision=HI, preferred_element_type=F32)


def gram_dot(left_matrix, right_matrix):
    return lax.dot_general(
        left_matrix, right_matrix, (((0,), (0,)), ((), ())), precision=HI, preferred_element_type=F32
    )


def cosine(x):
    n = jnp.round(x * 0.3183098861837907)
    r = x - n * 3.140625
    r = r - n * 9.67025756835938e-4
    r = r - n * 6.2771141529083251953e-7
    half = n * 0.5
    sign = 1.0 - 4.0 * (half - jnp.floor(half))
    s = r * r
    p = 2.08767569878681e-9
    for coef in (
        -2.755731922398589e-7,
        2.48015873015873e-5,
        -1.388888888888889e-3,
        4.166666666666667e-2,
        -0.5,
        1.0,
    ):
        p = p * s + coef
    return p * sign


def invert_small(pivots):
    size = len(pivots)
    held = [list(line) for line in pivots]
    for j in range(size):
        inverse = 1.0 / held[j][j]
        line = [inverse if m == j else held[j][m] * inverse for m in range(size)]
        for i in range(size):
            if i != j:
                factor = held[i][j]
                held[i] = [
                    -factor * line[m] if m == j else held[i][m] - factor * line[m] for m in range(size)
                ]
        held[j] = line
    return held


def invert_blocks(values):
    size = values[0].shape[0]
    many = [[value[t * 8 : t * 8 + 8, :] for t in range(size // 8)] for value in values]
    lane = lax.broadcasted_iota(jnp.int32, (8, size), 1)
    sub = lax.broadcasted_iota(jnp.int32, (8, size), 0)
    for j in range(0, size, GROUP):
        home, inner = divmod(j, 8)
        in_group = (lane >= j) & (lane < j + GROUP)
        for which, tiles in enumerate(many):
            rows = [
                jnp.broadcast_to(tiles[home][inner + k : inner + k + 1, :], (8, size)) for k in range(GROUP)
            ]
            pivots = invert_small(
                [[jnp.broadcast_to(row[:, j + m : j + m + 1], (8, size)) for m in range(GROUP)] for row in rows]
            )
            scaled = []
            for k in range(GROUP):
                line = pivots[k][0] * rows[0]
                for m in range(1, GROUP):
                    line = line + pivots[k][m] * rows[m]
                for m in range(GROUP):
                    line = jnp.where(lane == j + m, pivots[k][m], line)
                scaled.append(line)
            nxt = []
            for t, tile in enumerate(tiles):
                new = jnp.where(in_group, 0.0, tile)
                for k in range(GROUP):
                    new = new - jnp.broadcast_to(tile[:, j + k : j + k + 1], (8, size)) * scaled[k]
                if t == home:
                    for k in range(GROUP):
                        new = jnp.where(sub == inner + k, scaled[k], new)
                nxt.append(new)
            many[which] = nxt
    return [jnp.concatenate(tiles, axis=0) for tiles in many]


def spd_kernel(gram_ref, rhs_ref, out_ref, work):
    systems, total = gram_ref.shape[:2]
    size = BLOCK
    work[...] = gram_ref[...]
    out_ref[...] = rhs_ref[...]

    def step(k, carry):
        at = pl.ds(pl.multiple_of(k * size, size), size)
        inverses = invert_blocks([work[s, at, at] for s in range(systems)])
        for s in range(systems):
            inv = inverses[s]
            row_a = precise_dot(inv, work[s, at, :])
            row_x = precise_dot(inv, out_ref[s, at, :])
            for i in range(total // size):
                rows = pl.ds(i * size, size)
                left = jnp.where(k == i, 0.0, work[s, rows, at])
                work[s, rows, :] = work[s, rows, :] - precise_dot(left, row_a)
                out_ref[s, rows, :] = out_ref[s, rows, :] - precise_dot(left, row_x)
            work[s, at, :] = row_a
            out_ref[s, at, :] = row_x
        return carry

    lax.fori_loop(0, total // size, step, 0)


def spd_solve(gram_matrices, rhs_matrices):
    systems, total, cols = rhs_matrices.shape
    return pl.pallas_call(
        spd_kernel,
        out_shape=jax.ShapeDtypeStruct((systems, total, cols), F32),
        in_specs=[pl.BlockSpec(memory_space=pltpu.VMEM)] * 2,
        out_specs=pl.BlockSpec(memory_space=pltpu.VMEM),
        scratch_shapes=[pltpu.VMEM((systems, total, total), F32)],
        compiler_params=pltpu.CompilerParams(vmem_limit_bytes=24 * 2**20),
        cost_estimate=pl.CostEstimate(flops=2 * 10**10, bytes_accessed=3 * 2**20, transcendentals=0),
        name="spd",
    )(gram_matrices, rhs_matrices)


def reduce_kernel(n, groups, piece_ref, out_ref, inbox, full, sends, recvs):
    me, col = lax.axis_index("samp"), lax.axis_index("tgt")
    rows, cols = piece_ref.shape[0] // n, piece_ref.shape[1]
    peers = [lax.rem(me + step, n) for step in range(1, n)]
    others = [lax.rem(col + step, groups) for step in range(1, groups)]
    barrier = pltpu.get_barrier_semaphore()
    for peer in peers:
        pl.semaphore_signal(barrier, inc=1, device_id={"samp": peer}, device_id_type=MESH)
    for other in others:
        pl.semaphore_signal(barrier, inc=1, device_id={"tgt": other}, device_id_type=MESH)
    pl.semaphore_wait(barrier, n + groups - 2)

    def block(index):
        return pl.ds(pl.multiple_of(index * rows, rows), rows)

    scatter = []
    for slot, peer in enumerate(peers):
        copy = pltpu.make_async_remote_copy(
            src_ref=piece_ref.at[block(peer)],
            dst_ref=inbox.at[slot],
            send_sem=sends.at[slot],
            recv_sem=recvs.at[slot],
            device_id={"samp": peer},
            device_id_type=MESH,
        )
        copy.start()
        scatter.append(copy)
    total = piece_ref[block(me), :]
    for slot, copy in enumerate(scatter):
        copy.wait_recv()
        total = total + inbox[slot]
    full[col, block(me), :] = total

    spread = []
    for slot, peer in enumerate(peers):
        copy = pltpu.make_async_remote_copy(
            src_ref=full.at[col, block(me)],
            dst_ref=full.at[col, block(me)],
            send_sem=sends.at[n + slot],
            recv_sem=recvs.at[n + slot],
            device_id={"samp": peer},
            device_id_type=MESH,
        )
        copy.start()
        spread.append(copy)
    for copy in spread:
        copy.wait_recv()

    swap = []
    for slot, other in enumerate(others):
        copy = pltpu.make_async_remote_copy(
            src_ref=full.at[col],
            dst_ref=full.at[col],
            send_sem=sends.at[2 * n + slot],
            recv_sem=recvs.at[2 * n + slot],
            device_id={"tgt": other},
            device_id_type=MESH,
        )
        copy.start()
        swap.append(copy)
    for copy in swap:
        copy.wait_recv()
    for t in range(groups):
        out_ref[:, t * cols : (t + 1) * cols] = full[t]
    for copy in scatter + spread + swap:
        copy.wait_send()


def full_gram(piece, ident):
    n, groups = lax.axis_size("samp"), lax.axis_size("tgt")
    rows, cols = piece.shape
    return pl.pallas_call(
        functools.partial(reduce_kernel, n, groups),
        out_shape=jax.ShapeDtypeStruct((rows, groups * cols), F32),
        in_specs=[pl.BlockSpec(memory_space=pltpu.VMEM)],
        out_specs=pl.BlockSpec(memory_space=pltpu.VMEM),
        scratch_shapes=[
            pltpu.VMEM((n - 1, rows // n, cols), F32),
            pltpu.VMEM((groups, rows, cols), F32),
            pltpu.SemaphoreType.DMA((2 * n + groups,)),
            pltpu.SemaphoreType.DMA((2 * n + groups,)),
        ],
        compiler_params=pltpu.CompilerParams(
            collective_id=ident, has_side_effects=True, vmem_limit_bytes=16 * 2**20
        ),
        cost_estimate=pl.CostEstimate(flops=10**10, bytes_accessed=2 * 2**20, transcendentals=0),
        name=f"gram{ident}",
    )(piece)


def body(samples, omega, phase, right_side):
    col_count = right_side.shape[1]
    sample_total = samples.shape[0] * lax.axis_size("samp")
    col_offset = lax.axis_index("tgt") * col_count

    def own(matrix):
        return lax.dynamic_slice_in_dim(matrix, col_offset, col_count, 1)

    def wide(matrix):
        return lax.all_gather(matrix, "tgt", axis=1, tiled=True)

    right_cols = lax.all_gather(right_side.astype(BF16), "samp", axis=0, tiled=True)
    right_all = wide(right_side)
    gram_rr = full_gram(gram_dot(right_all, right_side), 0)
    feats = cosine(jnp.dot(samples, omega, preferred_element_type=F32) + phase).astype(BF16)

    projected = jnp.dot(feats, right_cols, preferred_element_type=F32).astype(BF16)
    lifted = lax.dot_general(feats, projected, (((0,), (0,)), ((), ())), preferred_element_type=F32)
    lifted_own = lax.psum_scatter(lifted, "samp", scatter_dimension=0, tiled=True) / sample_total
    proj_all = wide(projected)
    gram_py = full_gram(
        lax.dot_general(proj_all, projected, (((0,), (0,)), ((), ())), preferred_element_type=F32), 1
    )
    gram_pq = gram_py / sample_total + ridge * gram_rr
    unit = jnp.eye(gram_rr.shape[0], dtype=F32)
    solved = spd_solve(jnp.stack([gram_pq, gram_rr]), jnp.stack([gram_rr, unit]))
    alpha, gram_inverse = solved[0], solved[1]

    lifted_all = wide(lifted_own)
    resid_all = right_all - precise_dot(lifted_all + ridge * right_all, alpha)
    resid_own = own(resid_all)
    resid_cols = lax.all_gather(resid_own.astype(BF16), "samp", axis=0, tiled=True)
    gram_new = full_gram(gram_dot(resid_all, resid_own), 2)
    beta = precise_dot(gram_inverse, gram_new)
    direction_all = resid_all + precise_dot(right_all, beta)
    carried = precise_dot(proj_all.astype(F32), own(beta))

    second = (jnp.dot(feats, resid_cols, preferred_element_type=F32) + carried).astype(BF16)
    gram_two = full_gram(
        lax.dot_general(wide(second), second, (((0,), (0,)), ((), ())), preferred_element_type=F32)
        / sample_total
        + ridge * gram_dot(direction_all, own(direction_all)),
        3,
    )
    alpha_two = spd_solve(gram_two[None], own(gram_new)[None])[0]
    return precise_dot(right_all, own(alpha)) + precise_dot(direction_all, alpha_two)


def solution(mesh):
    placed = (P("samp", None), P(), P(), P("samp", "tgt"))
    return jax.shard_map(
        body, mesh=mesh, in_specs=placed, out_specs=P("samp", "tgt"), check_vma=False
    )
```

profile of v0, /device:TPU:1, one launch (start us, length us, event | category | flops | bytes accessed | tf_op | source)
XLA Modules:
  0.0 395.3 jit_solution(8044779731190441787)
XLA Ops:
  6.5 1.7 convert_element_type.27
  8.3 4.1 %fusion.3 = bf16[192,4096]{1,0:T(8,128)(2,1)S(1)} fusion(bf16[192,128]{1,0:T(8,128)(2,1)} %param.4, bf16[128,4096]{1,0:T(8,128)(2,1)S(1)} %copy-done, f32[4096]{0:T(1024)} %param.6), kind=kOutput, calls=%fused_computation.5 | convolution fusion | flops 224133120 | bytes 2686976 | tf_op jit(solution)/shard_map/dot_general | solution.py:245
  12.5 59.2 %all-gather.3.cloned.1.call-done = bf16[4096,256]{1,0:T(8,128)(2,1)} async-done(((bf16[256,256]{1,0:T(8,128)(2,1)}), bf16[4096,256]{1,0:T(8,128)(2,1)}) %all-gather.3.cloned.1.call-update) | async-done | bytes 2097168 | tf_op jit(solution)/shard_map/all_gather | solution.py:242
  71.6 2.2 convolution_convert_fusion
  73.8 2.7 fusion.28
  77.5 3.4 all_gather.20
  82.8 35.8 %gram0.1 = f32[512,512]{1,0:T(8,128)S(1)} custom-call(f32[512,256]{1,0:T(8,128)S(1)} %fusion.27.piece_ref), custom_call_target="tpu_custom_call" | custom-call | flops 10000000000 | bytes 2097152 | tf_op jit(solution)/shard_map/gram0/pallas_call | solution.py:212
  118.6 1.9 all_gather.19
  120.8 50.2 %gram1.1 = f32[512,512]{1,0:T(8,128)S(1)} custom-call(f32[512,256]{1,0:T(8,128)S(1)} %fusion.26.piece_ref), custom_call_target="tpu_custom_call" | custom-call | flops 10000000000 | bytes 2097152 | tf_op jit(solution)/shard_map/gram1/pallas_call | solution.py:212
  171.8 57.0 %spd.2 = f32[2,512,512]{2,1,0:T(8,128)S(1)} custom-call(f32[2,512,512]{2,1,0:T(8,128)S(1)} %get-tuple-element.6.gram_ref, f32[2,512,512]{2,1,0:T(8,128)S(1)} %get-tuple-element.5.rhs_ref), custom_call_target="tpu_custom_call" | custom-call | flops 20000000000 | bytes 3145728 | tf_op jit(solution)/shard_map/spd/pallas_call | solution.py:129
  228.9 1.2 broadcast_multiply_fusion
  230.0 2.4 all_gather.21
  232.4 2.3 convolution_subtract_fusion
  236.3 2.1 fusion.19.piece_ref
  238.4 35.4 %gram2.1 = f32[512,512]{1,0:T(8,128)S(1)} custom-call(f32[512,256]{1,0:T(8,128)S(1)} %fusion.19.piece_ref), custom_call_target="tpu_custom_call" | custom-call | flops 10000000000 | bytes 2097152 | tf_op jit(solution)/shard_map/gram2/pallas_call | solution.py:212
  274.6 1.8 fusion.8
  276.5 1.1 fusion.4
  277.6 1.8 fusion.17
  279.4 26.2 %all-gather.5.cloned.1.call-done = bf16[4096,256]{1,0:T(8,128)(2,1)} async-done(((bf16[256,256]{1,0:T(8,128)(2,1)}), bf16[4096,256]{1,0:T(8,128)(2,1)}) %all-gather.5.cloned.1.call-update) | async-done | bytes 2097168 | tf_op jit(solution)/shard_map/all_gather | solution.py:262
  305.6 2.3 fusion.29
  308.3 3.5 all_gather.23
  312.0 29.3 %gram3.1 = f32[512,512]{1,0:T(8,128)S(1)} custom-call(f32[512,256]{1,0:T(8,128)S(1)} %fusion.5.piece_ref), custom_call_target="tpu_custom_call" | custom-call | flops 10000000000 | bytes 2097152 | tf_op jit(solution)/shard_map/gram3/pallas_call | solution.py:212
  341.4 44.5 %spd.3 = f32[1,512,256]{2,1,0:T(8,128)S(1)} custom-call(f32[1,512,512]{2,1,0:T(8,128)S(1)} %bitcast.49, f32[1,512,256]{2,1,0:T(8,128)S(1)} %copy-done.2), custom_call_target="tpu_custom_call" | custom-call | flops 20000000000 | bytes 3145728 | tf_op jit(solution)/shard_map/spd/pallas_call | solution.py:129
  386.9 1.0 fusion.6
  (48 shorter events, 8.8 us)
Async XLA Ops:
  6.5 1.8 copy-start
  6.5 65.1 %all-gather.3.cloned.1.call-start = ((), (), s32[]{:S(2)}) async-start(), calls=%async_computation.1 | async-start | bytes 2228224 | tf_op jit(solution)/shard_map/all_gather | solution.py:242
  8.3 220.6 %reduce-scatter.2.cloned.1.call-start = ((), (), s32[]{:S(2)}) async-start(), calls=%async_computation.2 | async-start | bytes 4456448 | tf_op jit(solution)/shard_map/reduce_scatter | solution.py:249
  12.5 64.1 %copy-start.3 = (bf16[192,4096]{1,0:T(8,128)(2,1)}, bf16[192,4096]{1,0:T(8,128)(2,1)S(1)}, u32[]{:S(2)}) copy-start(bf16[192,4096]{1,0:T(8,128)(2,1)S(1)} %fusion.3) | copy-start | bytes 4718596
  76.5 1.0 copy-start.12
  76.6 229.0 %all-gather.5.cloned.1.call-start = ((), (), s32[]{:S(2)}) async-start(), calls=%async_computation.3 | async-start | bytes 2228224 | tf_op jit(solution)/shard_map/all_gather | solution.py:262
  80.9 0.8 copy-start.5
  228.8 45.8 %copy-start.1 = (f32[2,512,512]{2,1,0:T(8,128)}, f32[2,512,512]{2,1,0:T(8,128)S(1)}, u32[]{:S(2)}) copy-start(f32[2,512,512]{2,1,0:T(8,128)S(1)} %spd.2) | copy-start | bytes 6291460
  234.8 0.8 copy-start.10
  273.8 2.7 copy-start.6
  273.8 2.7 copy-start.11
  276.5 1.1 copy-start.8
  276.5 29.1 %copy-start.4 = (bf16[192,4096]{1,0:T(8,128)(2,1)S(1)}, bf16[192,4096]{1,0:T(8,128)(2,1)}, u32[]{:S(2)}) copy-start(bf16[192,4096]{1,0:T(8,128)(2,1)} %copy-done.3) | copy-start | bytes 4718596
  305.6 2.3 copy-start.9
  305.6 6.2 %copy-start.13 = (f32[512,256]{1,0:T(8,128)S(1)}, f32[512,256]{1,0:T(8,128)}, u32[]{:S(2)}) copy-start(f32[512,256]{1,0:T(8,128)} %fusion.17) | copy-start | bytes 1572868
  312.0 29.3 %copy-start.2 = (f32[1,512,256]{2,1,0:T(8,128)S(1)}, f32[1,512,256]{2,1,0:T(8,128)}, u32[]{:S(2)}) copy-start(f32[1,512,256]{2,1,0:T(8,128)} %dynamic-slice_bitcast_fusion.rhs_ref) | copy-start | bytes 1572868
  341.3 45.5 %slice-start = ((f32[2,512,512]{2,1,0:T(8,128)}), f32[1,512,512]{2,1,0:T(8,128)S(1)}, s32[]{:S(2)}) async-start(f32[2,512,512]{2,1,0:T(8,128)} %copy-done.1), calls=%async_computation.4 | async-start | bytes 2097152 | tf_op jit(solution)/shard_map/slice | solution.py:257
  341.4 45.5 %copy-start.7 = (f32[256,512]{1,0:T(8,128)S(1)}, f32[256,512]{1,0:T(8,128)}, u32[]{:S(2)}) copy-start(f32[256,512]{1,0:T(8,128)} %copy-done.5) | copy-start | bytes 1572868
Sparse Core Ops, SparseCore 0:
  10.1 61.4 all-gather.2
  76.7 117.8 reduce-scatter.1
  236.4 69.1 all-gather.4
where the time goes:
time: 396 us; the launch traced here: 395 us
  Pallas kernels  252 us (64%)
  waiting for transfers between devices  85.4 us (22%)
  matrix products  24.4 us (6%)
  between operations  13.4 us (3%)
  blocking collectives  11.2 us (3%)
  local copies, waits for them, and re-layouts  4.76 us (1%)
    pallas_call x4, Pallas kernels, full_gram(): pl.pallas_call(functools.partial(reduce_kernel, n, groups), out_shape=jax...  151 us
    pallas_call x2, Pallas kernels, spd_solve(): pl.pallas_call(spd_kernel, out_shape=jax.ShapeDtypeStruct((systems, total...  101 us
    all_gather x1, waiting for transfers between devices, body(): lax.all_gather(right_side.astype(BF16), 'samp', axis=0, tiled=True)  59.2 us
    all_gather x1, waiting for transfers between devices, body(): lax.all_gather(resid_own.astype(BF16), 'samp', axis=0, tiled=True)  26.2 us
    all_gather x4, blocking collectives, wide(): return lax.all_gather(matrix, 'tgt', axis=1, tiled=True)  11.2 us
  transfers between devices with their start and end apart: 3, of which 2 were waited for; matrix products, arithmetic and copies ran while one was open for 4% of the time, Pallas kernels for 45%

commit v1 on v0

v1 whole, which is shorter than its diff:
```python
import functools

import jax
import jax.numpy as jnp
from jax import lax
from jax.experimental import pallas as pl
from jax.experimental.pallas import tpu as pltpu
from jax.sharding import PartitionSpec as P

ridge = 1.0
HI = lax.Precision.HIGHEST
F32 = jnp.float32
BF16 = jnp.bfloat16
BLOCK = 128
GROUP = 8
PLANE = 4
MESH = pl.DeviceIdType.MESH
NN = (((1,), (0,)), ((), ()))
TN = (((0,), (0,)), ((), ()))
NT = (((1,), (1,)), ((), ()))
VMEM = pl.BlockSpec(memory_space=pltpu.VMEM)


def precise_dot(left_matrix, right_matrix):
    return jnp.dot(left_matrix, right_matrix, precision=HI, preferred_element_type=F32)


def dot(left, right, dims=NN):
    return lax.dot_general(left, right, dims, preferred_element_type=F32)


def halves(x):
    high = x.astype(BF16)
    return high, (x - high.astype(F32)).astype(BF16)


def dot_halves(left, right, dims=NN):
    return dot(left[0], right[0], dims) + (dot(left[0], right[1], dims) + dot(left[1], right[0], dims))


def cosine(x):
    turns = x * 0.15915494309189535
    f = turns - jnp.round(turns)
    s = f * f
    p = -21.071105627575776
    for coef in (
        58.790492120100176,
        -85.27162153429538,
        64.92865742103322,
        -19.738980355764014,
        0.999999210782322,
    ):
        p = p * s + coef
    return p


def sweep(held):
    size = len(held)
    at = lambda i, j: held[max(i, j)][min(i, j)]
    for p in range(size):
        inverse = 1.0 / held[p][p]
        column = [at(i, p) for i in range(size)]
        scaled = [c * inverse for c in column]
        for i in range(size):
            for j in range(i + 1):
                if i == p and j == p:
                    held[i][j] = -inverse
                elif i == p:
                    held[i][j] = scaled[j]
                elif j == p:
                    held[i][j] = scaled[i]
                else:
                    held[i][j] = held[i][j] - scaled[i] * column[j]
    return [[-at(i, j) for j in range(size)] for i in range(size)]


def invert_block(value):
    size = value.shape[0]
    tiles = [value[t * 8 : t * 8 + 8, :] for t in range(size // 8)]
    lane = lax.broadcasted_iota(jnp.int32, (8, size), 1)
    sub = lax.broadcasted_iota(jnp.int32, (8, size), 0)
    for g in range(size // GROUP):
        j = g * GROUP
        in_group = (lane >= j) & (lane < j + GROUP)
        home = tiles[g]
        spread = [jnp.broadcast_to(home[:, j + m : j + m + 1], (8, size)) for m in range(GROUP)]
        rows = [jnp.broadcast_to(home[k : k + 1, :], (8, size)) for k in range(GROUP)]
        pivots = sweep(
            [[jnp.broadcast_to(spread[m][k : k + 1, :], (8, size)) for m in range(k + 1)] for k in range(GROUP)]
        )
        scaled = []
        for k in range(GROUP):
            terms = [pivots[k][m] * rows[m] for m in range(GROUP)]
            while len(terms) > 1:
                terms = [terms[i] + terms[i + 1] for i in range(0, len(terms), 2)]
            line = terms[0]
            for m in range(GROUP):
                line = jnp.where(lane == j + m, pivots[k][m], line)
            scaled.append(line)
        nxt = []
        for t, tile in enumerate(tiles):
            if t == g:
                new = scaled[0]
                for k in range(1, GROUP):
                    new = jnp.where(sub == k, scaled[k], new)
            else:
                terms = [jnp.broadcast_to(tile[:, j + k : j + k + 1], (8, size)) * scaled[k] for k in range(GROUP)]
                while len(terms) > 1:
                    terms = [terms[i] + terms[i + 1] for i in range(0, len(terms), 2)]
                new = jnp.where(in_group, 0.0, tile) - terms[0]
            nxt.append(new)
        tiles = nxt
    return jnp.concatenate(tiles, axis=0)


def inverse_kernel(gram_ref, work):
    total = gram_ref.shape[0]
    size = BLOCK
    work[...] = gram_ref[...]

    def step(k, carry):
        at = pl.ds(pl.multiple_of(k * size, size), size)
        inv = invert_block(work[at, at])
        work[at, :] = precise_dot(inv, work[at, :])
        work[at, at] = inv
        row = work[at, :]
        for i in range(total // size):
            rows = pl.ds(i * size, size)
            block = work[rows, at]
            work[rows, at] = jnp.where(k == i, block, 0.0)
            work[rows, :] = work[rows, :] - precise_dot(jnp.where(k == i, 0.0, block), row)
        return carry

    lax.fori_loop(0, total // size, step, 0)


def inverse_of(gram):
    total = gram.shape[0]
    return pl.pallas_call(
        inverse_kernel,
        out_shape=jax.ShapeDtypeStruct((total, total), F32),
        in_specs=[VMEM],
        out_specs=VMEM,
        compiler_params=pltpu.CompilerParams(vmem_limit_bytes=16 * 2**20),
        cost_estimate=pl.CostEstimate(flops=2 * 10**10, bytes_accessed=2 * 2**20, transcendentals=0),
        name="inverse",
    )(gram)


def last_kernel(gram_ref, rhs_ref, right_ref, first_ref, direction_ref, out_ref, work, side):
    total = gram_ref.shape[0]
    size = BLOCK
    work[...] = gram_ref[...]
    side[...] = rhs_ref[...]

    def step(k, carry):
        at = pl.ds(pl.multiple_of(k * size, size), size)
        inv = invert_block(work[at, at])
        row_a = precise_dot(inv, work[at, :])
        row_x = precise_dot(inv, side[at, :])
        for i in range(total // size):
            rows = pl.ds(i * size, size)
            left = jnp.where(k == i, 0.0, work[rows, at])
            work[rows, :] = work[rows, :] - precise_dot(left, row_a)
            side[rows, :] = side[rows, :] - precise_dot(left, row_x)
        work[at, :] = row_a
        side[at, :] = row_x
        return carry

    lax.fori_loop(0, total // size, step, 0)
    out_ref[...] = dot_halves(halves(right_ref[...]), halves(first_ref[...])) + dot_halves(
        halves(direction_ref[...]), halves(side[...])
    )


def last_solve(gram, rhs, right_all, first, direction):
    total, cols = rhs.shape
    return pl.pallas_call(
        last_kernel,
        out_shape=jax.ShapeDtypeStruct((direction.shape[0], cols), F32),
        in_specs=[VMEM] * 5,
        out_specs=VMEM,
        scratch_shapes=[pltpu.VMEM((total, total), F32), pltpu.VMEM((total, cols), F32)],
        compiler_params=pltpu.CompilerParams(vmem_limit_bytes=24 * 2**20),
        cost_estimate=pl.CostEstimate(flops=2 * 10**10, bytes_accessed=3 * 2**20, transcendentals=0),
        name="last",
    )(gram, rhs, right_all, first, direction)


class Place:
    def __init__(self, n, groups):
        self.n, self.groups, self.lines = n, groups, n // PLANE
        self.me, self.col = lax.axis_index("samp"), lax.axis_index("tgt")
        self.inner = lax.rem(self.me, PLANE)
        self.line = lax.div(self.me, PLANE)
        self.over_x = self.me + 1 - 2 * lax.rem(self.me, 2)
        self.over_y = self.me + 2 - 4 * lax.div(self.inner, 2)
        self.inner_x = lax.rem(self.over_x, PLANE)
        self.inner_y = lax.rem(self.over_y, PLANE)
        self.along = [lax.rem(self.line + s, self.lines) * PLANE + self.inner for s in range(1, self.lines)]
        self.others = [lax.rem(self.col + s, groups) for s in range(1, groups)]

    def meet(self):
        barrier = pltpu.get_barrier_semaphore()
        for peer in [*self.along, self.over_x, self.over_y]:
            pl.semaphore_signal(barrier, inc=1, device_id={"samp": peer}, device_id_type=MESH)
        for other in self.others:
            pl.semaphore_signal(barrier, inc=1, device_id={"tgt": other}, device_id_type=MESH)
        pl.semaphore_wait(barrier, len(self.along) + 2 + len(self.others))

    def behind(self, s, inner):
        return lax.rem(self.line + self.lines - s, self.lines) * PLANE + inner


class Gather:
    def __init__(self, place, slab, rows, sends, recvs):
        self.place, self.slab, self.rows, self.sends, self.recvs = place, slab, rows, sends, recvs
        self.started = []
        self.z, self.x, self.y, self.d = {}, {}, {}, []

    def span(self, block, part=None):
        if part is None:
            return self.slab.at[pl.ds(pl.multiple_of(block * self.rows, self.rows), self.rows)]
        half = self.rows // 2
        return self.slab.at[pl.ds(pl.multiple_of(block * self.rows + part * half, half), half)]

    def send(self, ref, slot, peer):
        copy = pltpu.make_async_remote_copy(
            src_ref=ref,
            dst_ref=ref,
            send_sem=self.sends.at[slot],
            recv_sem=self.recvs.at[slot],
            device_id={"samp": peer},
            device_id_type=MESH,
        )
        copy.start()
        self.started.append(copy)
        return copy

    def across(self, s):
        p = self.place
        ref = self.span(p.behind(s, p.inner))
        base = p.lines + 4 * s
        self.x[s] = self.send(ref, base, p.over_x)
        self.y[s] = self.send(ref, base + 1, p.over_y)

    def open(self):
        p = self.place
        for s in range(1, p.lines):
            self.z[s] = self.send(self.span(p.me), s, p.along[s - 1])
        self.across(0)

    def relay(self, s):
        self.z[s].wait_recv()
        self.across(s)

    def corner(self, s):
        p = self.place
        base = p.lines + 4 * s
        self.x[s].wait_recv()
        self.d.append(self.send(self.span(p.behind(s, p.inner_x), 0), base + 2, p.over_y))
        self.y[s].wait_recv()
        self.d.append(self.send(self.span(p.behind(s, p.inner_y), 1), base + 3, p.over_x))

    def actions(self):
        steps = []
        for s in range(1, self.place.lines):
            steps.append(functools.partial(self.relay, s))
            steps.append(functools.partial(self.corner, s - 1))
        steps.append(functools.partial(self.corner, self.place.lines - 1))
        return steps

    def close(self):
        for copy in self.d:
            copy.wait_recv()

    def drain(self):
        for copy in self.started:
            copy.wait_send()


def room(groups):
    return (63 if groups > 2 else 40) * 2**20


def slots(n):
    return n // PLANE + 4 * (n // PLANE)


class Swap:
    def __init__(self, place, src, dst, sends, recvs, base, slotted=False):
        self.copies = []
        for i, other in enumerate(place.others):
            copy = pltpu.make_async_remote_copy(
                src_ref=src,
                dst_ref=dst.at[i] if slotted else dst,
                send_sem=sends.at[base + i],
                recv_sem=recvs.at[base + i],
                device_id={"tgt": other},
                device_id_type=MESH,
            )
            copy.start()
            self.copies.append(copy)

    def wait(self):
        for copy in self.copies:
            copy.wait_recv()

    def drain(self):
        for copy in self.copies:
            copy.wait_send()


def interleave(actions, work):
    done = 0
    for i, piece in enumerate(work):
        upto = (i + 1) * len(actions) // len(work)
        piece()
        for act in actions[done:upto]:
            act()
        done = upto


def beside(parts):
    return parts[0] if len(parts) == 1 else jnp.concatenate(parts, axis=1)


def first_kernel(
    n, groups, total_n,
    samples_ref, omega_ref, phase_ref, right_ref,
    gram_ref, mixed_ref, lifted_ref, part_ref, proj_ref, feats_ref,
    spots, flat, rights, projs, lifts, g_sends, g_recvs, s_sends, s_recvs,
):
    place = Place(n, groups)
    me, col = place.me, place.col
    rows, depth = samples_ref.shape
    feats, cols = right_ref.shape
    total_f = omega_ref.shape[1]
    mine = total_f // groups
    targets = groups * cols
    pieces, piece = spots.shape[0], spots.shape[1] // n
    slab = col if pieces > 1 else 0

    spots[slab, pl.ds(pl.multiple_of(me * piece, piece), piece), :] = samples_ref[
        pl.ds(pl.multiple_of(slab * piece, piece), piece), :
    ]
    rights[col, pl.ds(pl.multiple_of(me * feats, feats), feats), :] = right_ref[...].astype(BF16)
    place.meet()
    near = Gather(place, spots.at[slab], piece, g_sends.at[0], g_recvs.at[0])
    far = Gather(place, rights.at[col], feats, g_sends.at[1], g_recvs.at[1])
    near.open()
    far.open()

    tile = 256
    quarter = total_f // 4

    def own_features(part):
        def one(i, carry):
            at = pl.ds(pl.multiple_of(part * quarter + i * tile, tile), tile)
            feats_ref[:, at] = cosine(dot(samples_ref[...], omega_ref[:, at]) + phase_ref[:, at]).astype(BF16)
            return carry

        lax.fori_loop(0, quarter // tile, one, 0)

    interleave(near.actions(), [functools.partial(own_features, part) for part in range(4)])
    near.close()
    swaps = []
    if pieces > 1:
        swap = Swap(place, spots.at[col], spots.at[col], s_sends, s_recvs, 0)
        swaps.append(swap)
        swap.wait()

    def settle(b, carry):
        for t in range(pieces):
            flat[pl.ds(pl.multiple_of(b * rows + t * piece, piece), piece), :] = spots[
                t, pl.ds(pl.multiple_of(b * piece, piece), piece), :
            ]
        return carry

    lax.fori_loop(0, n, settle, 0)

    splits = 2
    tiles = total_n // tile // splits

    def lift_features(c, part):
        at = pl.ds(pl.multiple_of(col * mine + c * tile, tile), tile)
        weights = omega_ref[:, at].T
        shift = jnp.broadcast_to(phase_ref[:, at], (128, tile)).T
        shift = jnp.concatenate([shift] * (tile // 128), axis=1)
        down = pl.ds(c * tile, tile)

        def one(i, carry):
            over = pl.ds(pl.multiple_of((part * tiles + i) * tile, tile), tile)
            lifts[down, over] = cosine(dot(weights, flat[over, :], NT) + shift).astype(BF16)
            return carry

        lax.fori_loop(0, tiles, one, 0)

    interleave(
        far.actions(),
        [functools.partial(lift_features, c, part) for c in range(mine // tile) for part in range(splits)],
    )
    far.close()
    spread = Swap(place, rights.at[col], rights.at[col], s_sends, s_recvs, groups)
    swaps.append(spread)
    projs[col, pl.ds(pl.multiple_of(me * rows, rows), rows), :] = dot(feats_ref[...], rights[col]).astype(BF16)
    last = Gather(place, projs.at[col], rows, g_sends.at[2], g_recvs.at[2])
    last.open()

    chunk = 512
    spread.wait()

    def gram_piece(lo, hi):
        def one(i, carry):
            at = pl.ds(pl.multiple_of(i * chunk, chunk), chunk)
            block = beside([rights[t, at, :] for t in range(groups)])
            gram_ref[...] += dot(block, block, TN)
            return carry

        lax.fori_loop(lo, hi, one, 0)

    gram_ref[...] = jnp.zeros_like(gram_ref)
    count = total_f // chunk
    interleave(last.actions(), [functools.partial(gram_piece, i * count // 4, (i + 1) * count // 4) for i in range(4)])
    last.close()
    swap = Swap(place, projs.at[col], projs.at[col], s_sends, s_recvs, 2 * groups)
    swaps.append(swap)

    def lift(which):
        def one(i, carry):
            at = pl.ds(pl.multiple_of(i * chunk, chunk), chunk)
            lifted_ref[which, at, :] = dot(lifts[at, :], projs[which]) * (1.0 / total_n)
            return carry

        lax.fori_loop(0, mine // chunk, one, 0)

    lift(col)
    swap.wait()
    for other in place.others:
        lift(other)

    mixed_ref[...] = jnp.zeros_like(mixed_ref)

    def mix(i, carry):
        at = pl.ds(pl.multiple_of(i * chunk, chunk), chunk)
        block = beside([projs[t, at, :] for t in range(groups)])
        mixed_ref[...] += dot(block, block, TN)
        return carry

    lax.fori_loop(0, total_n // chunk, mix, 0)
    mixed_ref[...] = mixed_ref[...] * (1.0 / total_n) + ridge * gram_ref[...]
    own = pl.ds(pl.multiple_of(me * rows, rows), rows)
    for t in range(groups):
        part_ref[t] = rights[t, pl.ds(pl.multiple_of(col * mine, mine), mine), :]
        proj_ref[:, t * cols : (t + 1) * cols] = projs[t, own, :]
    for gather in (near, far, last):
        gather.drain()
    for swap in swaps:
        swap.drain()


def first_stage(samples, omega, phase, right_side):
    n, groups = lax.axis_size("samp"), lax.axis_size("tgt")
    rows, depth = samples.shape
    feats, cols = right_side.shape
    total_f = omega.shape[1]
    total_n, mine, targets = rows * n, total_f // groups, cols * groups
    pieces = groups if rows % (32 * groups) == 0 else 1
    return pl.pallas_call(
        functools.partial(first_kernel, n, groups, total_n),
        out_shape=[
            jax.ShapeDtypeStruct((targets, targets), F32),
            jax.ShapeDtypeStruct((targets, targets), F32),
            jax.ShapeDtypeStruct((groups, mine, cols), F32),
            jax.ShapeDtypeStruct((groups, mine, cols), BF16),
            jax.ShapeDtypeStruct((rows, targets), BF16),
            jax.ShapeDtypeStruct((rows, total_f), BF16),
        ],
        in_specs=[VMEM] * 4,
        out_specs=[VMEM] * 6,
        scratch_shapes=[
            pltpu.VMEM((pieces, total_n // pieces, depth), BF16),
            pltpu.VMEM((total_n, depth), BF16),
            pltpu.VMEM((groups, total_f, cols), BF16),
            pltpu.VMEM((groups, total_n, cols), BF16),
            pltpu.VMEM((mine, total_n), BF16),
            pltpu.SemaphoreType.DMA((3, slots(n))),
            pltpu.SemaphoreType.DMA((3, slots(n))),
            pltpu.SemaphoreType.DMA((3 * groups,)),
            pltpu.SemaphoreType.DMA((3 * groups,)),
        ],
        compiler_params=pltpu.CompilerParams(collective_id=0, has_side_effects=True, vmem_limit_bytes=room(groups)),
        cost_estimate=pl.CostEstimate(flops=10**11, bytes_accessed=2 * 2**20, transcendentals=0),
        name="first",
    )(samples, omega, phase.reshape(1, -1), right_side)


def second_kernel(
    n, groups, total_n,
    inverse_ref, gram_ref, lifted_ref, part_ref, proj_ref, feats_ref,
    first_ref, target_ref, final_ref, direction_ref,
    resid, sums, theirs, aside, away, projs, shared, g_sends, g_recvs, s_sends, s_recvs,
):
    place = Place(n, groups)
    me, col = place.me, place.col
    rows = feats_ref.shape[0]
    mine, cols = lifted_ref.shape[1:]
    targets = groups * cols
    chunk = 512
    place.meet()
    inverse = halves(inverse_ref[...])
    alpha = dot_halves(inverse, halves(gram_ref[...]))
    alpha_halves = halves(alpha)
    for t in range(groups):
        pl.when(col == t)(functools.partial(first_ref.__setitem__, Ellipsis, alpha[:, t * cols : (t + 1) * cols]))
    sums[...] = jnp.zeros_like(sums)
    aside[...] = jnp.zeros_like(aside)

    def one(i, carry):
        at = pl.ds(pl.multiple_of(i * chunk, chunk), chunk)
        right = beside([part_ref[t, at, :] for t in range(groups)]).astype(F32)
        image = halves(beside([lifted_ref[t, at, :] for t in range(groups)]) + ridge * right)
        left = right - dot_halves(image, alpha_halves)
        resid[at, :] = left
        pair = halves(left)
        sums[0] += dot_halves(image, pair, TN)
        sums[1] += dot_halves(pair, pair, TN)
        over = pl.ds(pl.multiple_of(col * mine + i * chunk, chunk), chunk)
        aside[...] += dot(feats_ref[:, over], pair[0])
        return carry

    lax.fori_loop(0, mine // chunk, one, 0)
    swaps = [
        Swap(place, sums.at[0], theirs.at[0], s_sends, s_recvs, 0, True),
        Swap(place, aside, away, s_sends, s_recvs, groups, True),
        Swap(place, sums.at[1], theirs.at[1], s_sends, s_recvs, 2 * groups, True),
    ]
    swaps[0].wait()

    def total(which):
        value = sums[which]
        for i in range(groups - 1):
            value = value + theirs[which, i]
        return value

    beta = -dot_halves(inverse, halves(total(0)))
    beta_halves = halves(beta)
    swaps[1].wait()
    value = aside[...]
    for i in range(groups - 1):
        value = value + away[i]
    value = value + dot(proj_ref[...], beta_halves[0]) + dot(proj_ref[...], beta_halves[1])
    own = pl.ds(pl.multiple_of(me * rows, rows), rows)
    for t in range(groups):
        pl.when(col == t)(
            functools.partial(projs.__setitem__, (t, own), value[:, t * cols : (t + 1) * cols].astype(BF16))
        )
    gather = Gather(place, projs.at[col], rows, g_sends, g_recvs)
    gather.open()
    final_ref[...] = jnp.zeros_like(final_ref)

    def turn(i):
        at = pl.ds(i * chunk, chunk)
        right = beside([part_ref[t, at, :] for t in range(groups)])
        line = resid[at, :] + dot(right, beta_halves[0]) + dot(right, beta_halves[1])
        resid[at, :] = line
        pair = halves(line)
        final_ref[...] += dot_halves(pair, pair, TN)

    interleave(gather.actions(), [functools.partial(turn, i) for i in range(mine // chunk)])
    swaps[2].wait()
    swaps.append(Swap(place, final_ref, shared, s_sends, s_recvs, 3 * groups, True))
    feats = direction_ref.shape[0]
    owners = n // groups
    source = lax.div(me, owners)
    held = pl.ds(pl.multiple_of(lax.rem(me, owners) * feats, feats), feats)
    new = total(1)
    for t in range(groups):
        pl.when(col == t)(functools.partial(target_ref.__setitem__, Ellipsis, new[:, t * cols : (t + 1) * cols]))

    def copies():
        return [
            pltpu.make_async_remote_copy(
                src_ref=resid.at[held],
                dst_ref=resid.at[pl.ds(mine, feats)],
                send_sem=s_sends.at[4 * groups + i],
                recv_sem=s_recvs.at[4 * groups],
                device_id={"tgt": other},
                device_id_type=MESH,
            )
            for i, other in enumerate(place.others)
        ]

    @pl.when(col == source)
    def _():
        for copy in copies():
            copy.start()

    gather.close()
    swaps.append(Swap(place, projs.at[col], projs.at[col], s_sends, s_recvs, 5 * groups))
    swaps[3].wait()
    swaps[3].drain()
    value = final_ref[...]
    for i in range(groups - 1):
        value = value + shared[i]
    final_ref[...] = ridge * value
    swaps[4].wait()

    def mix(i, carry):
        at = pl.ds(pl.multiple_of(i * chunk, chunk), chunk)
        block = beside([projs[t, at, :] for t in range(groups)])
        final_ref[...] += dot(block, block, TN) * (1.0 / total_n)
        return carry

    lax.fori_loop(0, total_n // chunk, mix, 0)

    @pl.when(col == source)
    def _():
        direction_ref[...] = resid[held, :]
        for copy in copies():
            copy.wait_send()

    @pl.when(col != source)
    def _():
        copies()[0].wait_recv()
        direction_ref[...] = resid[pl.ds(mine, feats), :]

    gather.drain()
    for swap in swaps[:3] + swaps[4:]:
        swap.drain()


def second_stage(inverse, gram, lifted, part, proj, feats_own, feats):
    n, groups = lax.axis_size("samp"), lax.axis_size("tgt")
    _, mine, cols = lifted.shape
    rows = feats_own.shape[0]
    total_n, targets = rows * n, cols * groups
    return pl.pallas_call(
        functools.partial(second_kernel, n, groups, total_n),
        out_shape=[
            jax.ShapeDtypeStruct((targets, cols), F32),
            jax.ShapeDtypeStruct((targets, cols), F32),
            jax.ShapeDtypeStruct((targets, targets), F32),
            jax.ShapeDtypeStruct((feats, targets), F32),
        ],
        in_specs=[VMEM] * 6,
        out_specs=[VMEM] * 4,
        scratch_shapes=[
            pltpu.VMEM((mine + feats, targets), F32),
            pltpu.VMEM((2, targets, targets), F32),
            pltpu.VMEM((2, max(groups - 1, 1), targets, targets), F32),
            pltpu.VMEM((rows, targets), F32),
            pltpu.VMEM((max(groups - 1, 1), rows, targets), F32),
            pltpu.VMEM((groups, total_n, cols), BF16),
            pltpu.VMEM((max(groups - 1, 1), targets, targets), F32),
            pltpu.SemaphoreType.DMA((slots(n),)),
            pltpu.SemaphoreType.DMA((slots(n),)),
            pltpu.SemaphoreType.DMA((6 * groups,)),
            pltpu.SemaphoreType.DMA((6 * groups,)),
        ],
        compiler_params=pltpu.CompilerParams(collective_id=1, has_side_effects=True, vmem_limit_bytes=room(groups)),
        cost_estimate=pl.CostEstimate(flops=10**11, bytes_accessed=2 * 2**20, transcendentals=0),
        name="second",
    )(inverse, gram, lifted, part, proj, feats_own)


def body(samples, omega, phase, right_side):
    gram, mixed, lifted, part, proj, feats_own = first_stage(samples, omega, phase, right_side)
    inverse = inverse_of(mixed)
    first, target, final, direction = second_stage(
        inverse, gram, lifted, part, proj, feats_own, right_side.shape[0]
    )
    right_all = lax.all_gather(right_side, "tgt", axis=1, tiled=True)
    return last_solve(final, target, right_all, first, direction)


def solution(mesh):
    placed = (P("samp", None), P(), P(), P("samp", "tgt"))
    return jax.shard_map(
        body, mesh=mesh, in_specs=placed, out_specs=P("samp", "tgt"), check_vma=False
    )
```

time: 396 us -> 203 us (0.51)
  waiting for transfers between devices: 85.4 us -> 0 us
  Pallas kernels: 252 us -> 197 us
  matrix products: 24.4 us -> 0 us
  between operations: 13.4 us -> 0.05 us
  blocking collectives: 11.2 us -> 2.18 us
    all_gather x2 -> x0, waiting for transfers between devices: 85.4 us -> none  [the longest x1 59.2 us: body(): lax.all_gather(right_side.astype(BF16), 'samp', axis=0, tiled=True)]
    pallas_call x6 -> x4, Pallas kernels: 252 us -> 197 us  [the longest x1 84.7 us: first_stage(): pl.pallas_call(functools.partial(first_kernel, n, groups, total_n), out_s...]
    dot_general x15 -> x0, matrix products: 24.4 us -> none  [the longest x6 7.67 us: precise_dot(): jnp.dot(left_matrix, right_matrix, precision=HI, preferred_element_type=F32)]
    all_gather x4 -> x1, blocking collectives: 11.2 us -> 2.18 us  [body(): right_all = lax.all_gather(right_side, 'tgt', axis=1, tiled=True)]
  transfers between devices with their start and end apart: 3 -> 0, of which waited for: 2 -> 0; matrix products, arithmetic and copies ran while one was open for 4% -> 0% of each run, Pallas kernels for 45% -> 0%
where the time goes in v1:
time: 203 us
  Pallas kernels  197 us (97%)
  local copies, waits for them, and re-layouts  3.69 us (2%)
  blocking collectives  2.18 us (1%)
    pallas_call x1, Pallas kernels, first_stage(): pl.pallas_call(functools.partial(first_kernel, n, groups, total_n), out_s...  84.7 us
    pallas_call x1, Pallas kernels, second_stage(): pl.pallas_call(functools.partial(second_kernel, n, groups, total_n), out_...  47.1 us
    pallas_call x1, Pallas kernels, last_solve(): pl.pallas_call(last_kernel, out_shape=jax.ShapeDtypeStruct((direction.sha...  34 us
    pallas_call x1, Pallas kernels, inverse_of(): pl.pallas_call(inverse_kernel, out_shape=jax.ShapeDtypeStruct((total, tot...  31 us

profile of v1, /device:TPU:1, one launch (start us, length us, event | category | flops | bytes accessed | tf_op | source)
XLA Modules:
  0.0 202.8 jit_solution(5193399472457111162)
XLA Ops:
  0.0 0.0 copy-start
  0.0 0.9 copy-done
  1.0 0.0 copy-start.2
  1.0 1.2 copy-done.2
  2.2 0.0 copy-start.3
  2.2 0.8 copy-done.3
  3.0 0.0 copy-start.4
  3.0 0.7 copy-done.4
  3.7 84.7 %first.1 = (f32[512,512]{1,0:T(8,128)S(1)}, f32[512,512]{1,0:T(8,128)S(1)}, f32[2,2048,256]{2,1,0:T(8,128)S(1)}, bf16[2,2048,256]{2,1,0:T(8,128)(2,1)S(1)}, bf16...) custom-call(bf16[192,128]{1,0:T(8,128)(2,1)S(1)} %copy-done.3, bf16[128,4096]{1,0:T(8,128)(2,1)S(1)} %copy-done.2, ...), custom_call_target="tpu_custom_call" | custom-call | flops 99999997952 | bytes 2097152 | tf_op jit(solution)/shard_map/first/pallas_call | solution.py:469
  88.4 31.0 %inverse.1.inverse_ref = f32[512,512]{1,0:T(8,128)S(1)} custom-call(f32[512,512]{1,0:T(8,128)S(1)} %get-tuple-element.15.gram_ref), custom_call_target="tpu_custom_call" | custom-call | flops 20000000000 | bytes 2097152 | tf_op jit(solution)/shard_map/inverse/pallas_call | solution.py:139
  119.5 0.0 copy-start.1
  119.5 47.1 %second.1 = (f32[512,256]{1,0:T(8,128)S(1)}, f32[512,256]{1,0:T(8,128)S(1)}, f32[512,512]{1,0:T(8,128)S(1)}, f32[256,512]{1,0:T(8,128)S(1)}) custom-call(f32[512,512]{1,0:T(8,128)S(1)} %inverse.1.inverse_ref, f32[512,512]{1,0:T(8,128)S(1)} %get-tuple-element.16.gram_ref, f32[2,2048,256]{2,1,0:T(8,128)S(1)} %get-tuple-element.17.lifted_ref, ...), custom_call_target="tpu_custom_call" | custom-call | flops 99999997952 | bytes 2097152 | tf_op jit(solution)/shard_map/second/pallas_call | solution.py:638
  166.6 0.0 copy-done.1
  166.6 2.2 %all_gather.3.right_ref = f32[256,512]{1,0:T(8,128)S(1)} all-gather(f32[256,256]{1,0:T(8,128)S(1)} %copy-done.1), channel_id=1, replica_groups=mesh['samp'=16,'tgt'=2] {'tgt'}, dimensions={1}, use_global_device_ids=true | all-gather | bytes 786432 | tf_op jit(solution)/shard_map/all_gather | solution.py:673
  168.8 34.0 %last.1 = f32[256,256]{1,0:T(8,128)} custom-call(f32[512,512]{1,0:T(8,128)S(1)} %get-tuple-element.21.gram_ref, f32[512,256]{1,0:T(8,128)S(1)} %get-tuple-element.22.rhs_ref, f32[256,512]{1,0:T(8,128)S(1)} %all_gather.3.right_ref, f32[512,256]{1,0:T(8,128)S(1)} %get-tuple-element.23.first_ref, f32[256,512]{1,0:T(8,128)S(1)} %get-tuple-element.24.direction_ref), custom_call_target="tpu_custom_call" | custom-call | flops 20000000000 | bytes 3145728 | tf_op jit(solution)/shard_map/last/pallas_call | solution.py:178
Async XLA Ops:
  0.0 0.9 copy-start
  1.0 1.2 copy-start.2
  2.2 0.8 copy-start.3
  3.0 0.7 copy-start.4
  119.5 47.1 %copy-start.1 = (f32[256,256]{1,0:T(8,128)S(1)}, f32[256,256]{1,0:T(8,128)}, u32[]{:S(2)}) copy-start(f32[256,256]{1,0:T(8,128)} %right_ref.1) | copy-start | bytes 786436

commit v2 on v1

--- a/solution.py
+++ b/solution.py
@@ -57,20 +57,23 @@
 def sweep(held):
     size = len(held)
     at = lambda i, j: held[max(i, j)][min(i, j)]
-    for p in range(size):
-        inverse = 1.0 / held[p][p]
-        column = [at(i, p) for i in range(size)]
-        scaled = [c * inverse for c in column]
-        for i in range(size):
-            for j in range(i + 1):
-                if i == p and j == p:
-                    held[i][j] = -inverse
-                elif i == p:
-                    held[i][j] = scaled[j]
-                elif j == p:
-                    held[i][j] = scaled[i]
-                else:
-                    held[i][j] = held[i][j] - scaled[i] * column[j]
+    for p in range(0, size, 2):
+        q = p + 1
+        a, b, c = held[p][p], held[q][p], held[q][q]
+        scale = 1.0 / (a * c - b * b)
+        pp, pq, qq = c * scale, b * scale, a * scale
+        first, second = [at(i, p) for i in range(size)], [at(i, q) for i in range(size)]
+        rest = [i for i in range(size) if i not in (p, q)]
+        left = {i: first[i] * pp - second[i] * pq for i in rest}
+        right = {i: second[i] * qq - first[i] * pq for i in rest}
+        for i in rest:
+            for j in rest:
+                if j <= i:
+                    held[i][j] = held[i][j] - (left[i] * first[j] + right[i] * second[j])
+        for i in rest:
+            held[max(i, p)][min(i, p)] = left[i]
+            held[max(i, q)][min(i, q)] = right[i]
+        held[p][p], held[q][p], held[q][q] = -pp, pq, -qq
     return [[-at(i, j) for j in range(size)] for i in range(size)]
 
 
@@ -84,7 +87,10 @@
         in_group = (lane >= j) & (lane < j + GROUP)
         home = tiles[g]
         spread = [jnp.broadcast_to(home[:, j + m : j + m + 1], (8, size)) for m in range(GROUP)]
-        rows = [jnp.broadcast_to(home[k : k + 1, :], (8, size)) for k in range(GROUP)]
+        rows = [
+            jnp.where(in_group, jnp.where(lane == j + k, 1.0, 0.0), jnp.broadcast_to(home[k : k + 1, :], (8, size)))
+            for k in range(GROUP)
+        ]
         pivots = sweep(
             [[jnp.broadcast_to(spread[m][k : k + 1, :], (8, size)) for m in range(k + 1)] for k in range(GROUP)]
         )
@@ -93,10 +99,7 @@
             terms = [pivots[k][m] * rows[m] for m in range(GROUP)]
             while len(terms) > 1:
                 terms = [terms[i] + terms[i + 1] for i in range(0, len(terms), 2)]
-            line = terms[0]
-            for m in range(GROUP):
-                line = jnp.where(lane == j + m, pivots[k][m], line)
-            scaled.append(line)
+            scaled.append(terms[0])
         nxt = []
         for t, tile in enumerate(tiles):
             if t == g:
@@ -113,25 +116,40 @@
     return jnp.concatenate(tiles, axis=0)
 
 
-def inverse_kernel(gram_ref, work):
+def inverse_kernel(gram_ref, work, row, column):
     total = gram_ref.shape[0]
     size = BLOCK
-    work[...] = gram_ref[...]
+    count = total // size
+    scale = 1.0 / jnp.max(gram_ref[...])
+    work[...] = gram_ref[...] * scale
+    row[...] = jnp.zeros_like(row)
+    column[...] = jnp.zeros_like(column)
 
     def step(k, carry):
         at = pl.ds(pl.multiple_of(k * size, size), size)
         inv = invert_block(work[at, at])
-        work[at, :] = precise_dot(inv, work[at, :])
+        for i in range(1, count):
+            rows = pl.ds(pl.multiple_of(lax.rem(k + i, count) * size, size), size)
+            work[rows, :] = work[rows, :] - precise_dot(column[rows, :], row[...])
+        new = precise_dot(inv, work[at, :])
+        for i in range(1, count):
+            rows = pl.ds(pl.multiple_of(lax.rem(k + i, count) * size, size), size)
+            column[rows, :] = work[rows, at]
+            work[rows, at] = jnp.zeros((size, size), F32)
+        work[at, :] = new
         work[at, at] = inv
-        row = work[at, :]
-        for i in range(total // size):
-            rows = pl.ds(i * size, size)
-            block = work[rows, at]
-            work[rows, at] = jnp.where(k == i, block, 0.0)
-            work[rows, :] = work[rows, :] - precise_dot(jnp.where(k == i, 0.0, block), row)
+        row[...] = new
+        row[:, at] = inv
+        soon = pl.ds(pl.multiple_of(lax.rem(k + 1, count) * size, size), size)
+        work[soon, :] = work[soon, :] - precise_dot(column[soon, :], row[...])
+        column[soon, :] = jnp.zeros((size, size), F32)
+        column[at, :] = jnp.zeros((size, size), F32)
         return carry
 
-    lax.fori_loop(0, total // size, step, 0)
+    lax.fori_loop(0, count, step, 0)
+    for i in range(count):
+        rows = pl.ds(i * size, size)
+        work[rows, :] = (work[rows, :] - precise_dot(column[rows, :], row[...])) * scale
 
 
 def inverse_of(gram):
@@ -141,36 +159,47 @@
         out_shape=jax.ShapeDtypeStruct((total, total), F32),
         in_specs=[VMEM],
         out_specs=VMEM,
+        scratch_shapes=[pltpu.VMEM((BLOCK, total), F32), pltpu.VMEM((total, BLOCK), F32)],
         compiler_params=pltpu.CompilerParams(vmem_limit_bytes=16 * 2**20),
         cost_estimate=pl.CostEstimate(flops=2 * 10**10, bytes_accessed=2 * 2**20, transcendentals=0),
         name="inverse",
     )(gram)
 
 
-def last_kernel(gram_ref, rhs_ref, right_ref, first_ref, direction_ref, out_ref, work, side):
-    total = gram_ref.shape[0]
+def last_kernel(gram_ref, rhs_ref, right_ref, first_ref, direction_ref, out_ref, work, row, column):
+    total, cols = rhs_ref.shape
     size = BLOCK
-    work[...] = gram_ref[...]
-    side[...] = rhs_ref[...]
+    count = total // size
+    scale = 1.0 / jnp.max(gram_ref[...])
+    work[:, :total] = gram_ref[...] * scale
+    work[:, total:] = rhs_ref[...] * scale
+    row[...] = jnp.zeros_like(row)
+    column[...] = jnp.zeros_like(column)
+    out_ref[...] = dot_halves(halves(right_ref[...]), halves(first_ref[...]))
 
     def step(k, carry):
         at = pl.ds(pl.multiple_of(k * size, size), size)
         inv = invert_block(work[at, at])
-        row_a = precise_dot(inv, work[at, :])
-        row_x = precise_dot(inv, side[at, :])
-        for i in range(total // size):
-            rows = pl.ds(i * size, size)
-            left = jnp.where(k == i, 0.0, work[rows, at])
-            work[rows, :] = work[rows, :] - precise_dot(left, row_a)
-            side[rows, :] = side[rows, :] - precise_dot(left, row_x)
-        work[at, :] = row_a
-        side[at, :] = row_x
+        for i in range(1, count):
+            rows = pl.ds(pl.multiple_of(lax.rem(k + i, count) * size, size), size)
+            work[rows, :] = work[rows, :] - precise_dot(column[rows, :], row[...])
+        new = precise_dot(inv, work[at, :])
+        for i in range(1, count):
+            rows = pl.ds(pl.multiple_of(lax.rem(k + i, count) * size, size), size)
+            column[rows, :] = work[rows, at]
+        work[at, :] = new
+        row[...] = new
+        soon = pl.ds(pl.multiple_of(lax.rem(k + 1, count) * size, size), size)
+        work[soon, :] = work[soon, :] - precise_dot(column[soon, :], row[...])
+        column[soon, :] = jnp.zeros((size, size), F32)
+        column[at, :] = jnp.zeros((size, size), F32)
         return carry
 
-    lax.fori_loop(0, total // size, step, 0)
-    out_ref[...] = dot_halves(halves(right_ref[...]), halves(first_ref[...])) + dot_halves(
-        halves(direction_ref[...]), halves(side[...])
-    )
+    lax.fori_loop(0, count, step, 0)
+    for i in range(count):
+        rows = pl.ds(i * size, size)
+        work[rows, total:] = work[rows, total:] - precise_dot(column[rows, :], row[:, total:])
+    out_ref[...] += dot_halves(halves(direction_ref[...]), halves(work[:, total:]))
 
 
 def last_solve(gram, rhs, right_all, first, direction):
@@ -180,7 +209,11 @@
         out_shape=jax.ShapeDtypeStruct((direction.shape[0], cols), F32),
         in_specs=[VMEM] * 5,
         out_specs=VMEM,
-        scratch_shapes=[pltpu.VMEM((total, total), F32), pltpu.VMEM((total, cols), F32)],
+        scratch_shapes=[
+            pltpu.VMEM((total, total + cols), F32),
+            pltpu.VMEM((BLOCK, total + cols), F32),
+            pltpu.VMEM((total, BLOCK), F32),
+        ],
         compiler_params=pltpu.CompilerParams(vmem_limit_bytes=24 * 2**20),
         cost_estimate=pl.CostEstimate(flops=2 * 10**10, bytes_accessed=3 * 2**20, transcendentals=0),
         name="last",
@@ -200,13 +233,15 @@
         self.along = [lax.rem(self.line + s, self.lines) * PLANE + self.inner for s in range(1, self.lines)]
         self.others = [lax.rem(self.col + s, groups) for s in range(1, groups)]
 
-    def meet(self):
+    def greet(self):
         barrier = pltpu.get_barrier_semaphore()
         for peer in [*self.along, self.over_x, self.over_y]:
             pl.semaphore_signal(barrier, inc=1, device_id={"samp": peer}, device_id_type=MESH)
         for other in self.others:
             pl.semaphore_signal(barrier, inc=1, device_id={"tgt": other}, device_id_type=MESH)
-        pl.semaphore_wait(barrier, len(self.along) + 2 + len(self.others))
+
+    def meet(self):
+        pl.semaphore_wait(pltpu.get_barrier_semaphore(), len(self.along) + 2 + len(self.others))
 
     def behind(self, s, inner):
         return lax.rem(self.line + self.lines - s, self.lines) * PLANE + inner
@@ -215,8 +250,8 @@
 class Gather:
     def __init__(self, place, slab, rows, sends, recvs):
         self.place, self.slab, self.rows, self.sends, self.recvs = place, slab, rows, sends, recvs
-        self.started = []
-        self.z, self.x, self.y, self.d = {}, {}, {}, []
+        self.started, self.mirrors = [], {}
+        self.z, self.x, self.y, self.d = {}, {}, {}, {}
 
     def span(self, block, part=None):
         if part is None:
@@ -244,10 +279,13 @@
         self.x[s] = self.send(ref, base, p.over_x)
         self.y[s] = self.send(ref, base + 1, p.over_y)
 
-    def open(self):
+    def along(self):
         p = self.place
         for s in range(1, p.lines):
             self.z[s] = self.send(self.span(p.me), s, p.along[s - 1])
+
+    def open(self):
+        self.along()
         self.across(0)
 
     def relay(self, s):
@@ -258,25 +296,45 @@
         p = self.place
         base = p.lines + 4 * s
         self.x[s].wait_recv()
-        self.d.append(self.send(self.span(p.behind(s, p.inner_x), 0), base + 2, p.over_y))
+        one = self.send(self.span(p.behind(s, p.inner_x), 0), base + 2, p.over_y)
         self.y[s].wait_recv()
-        self.d.append(self.send(self.span(p.behind(s, p.inner_y), 1), base + 3, p.over_x))
-
-    def actions(self):
-        steps = []
-        for s in range(1, self.place.lines):
+        self.d[s] = [one, self.send(self.span(p.behind(s, p.inner_y), 1), base + 3, p.over_x)]
+
+    def line(self, s):
+        size = PLANE * self.rows
+        first = lax.rem(self.place.line + self.place.lines - s, self.place.lines)
+        return pl.ds(pl.multiple_of(first * size, size), size)
+
+    def finish(self, s, mirror=None):
+        for copy in self.d[s]:
+            copy.wait_recv()
+        if mirror is not None:
+            sends, recvs, base = mirror
+            ref = self.slab.at[self.line(s)]
+            self.mirrors[s] = Swap(self.place, ref, ref, sends, recvs, base + s * self.place.groups)
+
+    def actions(self, mirror=None):
+        steps, lines = [], self.place.lines
+        for s in range(1, lines):
             steps.append(functools.partial(self.relay, s))
             steps.append(functools.partial(self.corner, s - 1))
-        steps.append(functools.partial(self.corner, self.place.lines - 1))
+            if mirror is not None and s > 1:
+                steps.append(functools.partial(self.finish, s - 2, mirror))
+        steps.append(functools.partial(self.corner, lines - 1))
+        if mirror is not None:
+            for s in range(max(lines - 2, 0), lines):
+                steps.append(functools.partial(self.finish, s, mirror))
         return steps
 
     def close(self):
-        for copy in self.d:
-            copy.wait_recv()
+        for s in range(self.place.lines):
+            self.finish(s)
 
     def drain(self):
         for copy in self.started:
             copy.wait_send()
+        for swap in self.mirrors.values():
+            swap.drain()
 
 
 def room(groups):
@@ -311,10 +369,13 @@
             copy.wait_send()
 
 
-def interleave(actions, work):
-    done = 0
+def interleave(actions, work, lead=0):
+    done = min(lead, len(actions))
+    for act in actions[:done]:
+        act()
+    rest = len(actions) - done
     for i, piece in enumerate(work):
-        upto = (i + 1) * len(actions) // len(work)
+        upto = len(actions) - rest + (i + 1) * rest // len(work)
         piece()
         for act in actions[done:upto]:
             act()
@@ -327,48 +388,58 @@
 
 def first_kernel(
     n, groups, total_n,
-    samples_ref, omega_ref, phase_ref, right_ref,
-    gram_ref, mixed_ref, lifted_ref, part_ref, proj_ref, feats_ref,
-    spots, flat, rights, projs, lifts, g_sends, g_recvs, s_sends, s_recvs,
+    samples_hbm, omega_hbm, phase_hbm, right_hbm,
+    gram_ref, mixed_ref, lifted_ref, part_ref, proj_ref, feats_ref, wide_ref,
+    samples_ref, omega_ref, phase_ref, wides, spots, flat, rights, projs, lifts,
+    loads, g_sends, g_recvs, s_sends, s_recvs, m_sends, m_recvs,
 ):
     place = Place(n, groups)
     me, col = place.me, place.col
     rows, depth = samples_ref.shape
-    feats, cols = right_ref.shape
+    feats, cols = wides.shape[1:]
     total_f = omega_ref.shape[1]
     mine = total_f // groups
-    targets = groups * cols
     pieces, piece = spots.shape[0], spots.shape[1] // n
     slab = col if pieces > 1 else 0
 
+    fetches = [
+        pltpu.make_async_copy(src, dst, loads.at[i])
+        for i, (src, dst) in enumerate(
+            [(samples_hbm, samples_ref), (right_hbm, wides.at[col]), (omega_hbm, omega_ref), (phase_hbm, phase_ref)]
+        )
+    ]
+    for fetch in fetches:
+        fetch.start()
+    place.greet()
+    fetches[0].wait()
     spots[slab, pl.ds(pl.multiple_of(me * piece, piece), piece), :] = samples_ref[
         pl.ds(pl.multiple_of(slab * piece, piece), piece), :
     ]
-    rights[col, pl.ds(pl.multiple_of(me * feats, feats), feats), :] = right_ref[...].astype(BF16)
+    fetches[1].wait()
+    rights[col, pl.ds(pl.multiple_of(me * feats, feats), feats), :] = wides[col].astype(BF16)
+    fetches[2].wait()
+    fetches[3].wait()
+
+    tile = 256
+
+    def own_features(i, carry):
+        at = pl.ds(pl.multiple_of(i * tile, tile), tile)
+        feats_ref[:, at] = cosine(dot(samples_ref[...], omega_ref[:, at]) + phase_ref[:, at]).astype(BF16)
+        return carry
+
+    lax.fori_loop(0, total_f // tile, own_features, 0)
     place.meet()
     near = Gather(place, spots.at[slab], piece, g_sends.at[0], g_recvs.at[0])
     far = Gather(place, rights.at[col], feats, g_sends.at[1], g_recvs.at[1])
     near.open()
     far.open()
-
-    tile = 256
-    quarter = total_f // 4
-
-    def own_features(part):
-        def one(i, carry):
-            at = pl.ds(pl.multiple_of(part * quarter + i * tile, tile), tile)
-            feats_ref[:, at] = cosine(dot(samples_ref[...], omega_ref[:, at]) + phase_ref[:, at]).astype(BF16)
-            return carry
-
-        lax.fori_loop(0, quarter // tile, one, 0)
-
-    interleave(near.actions(), [functools.partial(own_features, part) for part in range(4)])
+    swaps = [Swap(place, wides.at[col], wides.at[col], s_sends, s_recvs, 0)]
+    for act in near.actions():
+        act()
     near.close()
-    swaps = []
     if pieces > 1:
-        swap = Swap(place, spots.at[col], spots.at[col], s_sends, s_recvs, 0)
-        swaps.append(swap)
-        swap.wait()
+        swaps.append(Swap(place, spots.at[col], spots.at[col], s_sends, s_recvs, groups))
+        swaps[-1].wait()
 
     def settle(b, carry):
         for t in range(pieces):
@@ -379,10 +450,10 @@
 
     lax.fori_loop(0, n, settle, 0)
 
-    splits = 2
-    tiles = total_n // tile // splits
-
-    def lift_features(c, part):
+    tiles = total_n // tile
+    batch = 3 if tiles % 3 == 0 else 1
+
+    def lift_features(c):
         at = pl.ds(pl.multiple_of(col * mine + c * tile, tile), tile)
         weights = omega_ref[:, at].T
         shift = jnp.broadcast_to(phase_ref[:, at], (128, tile)).T
@@ -390,25 +461,24 @@
         down = pl.ds(c * tile, tile)
 
         def one(i, carry):
-            over = pl.ds(pl.multiple_of((part * tiles + i) * tile, tile), tile)
-            lifts[down, over] = cosine(dot(weights, flat[over, :], NT) + shift).astype(BF16)
+            for b in range(batch):
+                over = pl.ds(pl.multiple_of((i * batch + b) * tile, tile), tile)
+                lifts[down, over] = cosine(dot(weights, flat[over, :], NT) + shift).astype(BF16)
             return carry
 
-        lax.fori_loop(0, tiles, one, 0)
-
-    interleave(
-        far.actions(),
-        [functools.partial(lift_features, c, part) for c in range(mine // tile) for part in range(splits)],
-    )
+        lax.fori_loop(0, tiles // batch, one, 0)
+
+    work = [functools.partial(lift_features, c) for c in range(mine // tile)]
+    early = len(work) * 5 // 8
+    interleave(far.actions(), work[:early], 3)
     far.close()
-    spread = Swap(place, rights.at[col], rights.at[col], s_sends, s_recvs, groups)
+    spread = Swap(place, rights.at[col], rights.at[col], s_sends, s_recvs, 2 * groups)
     swaps.append(spread)
     projs[col, pl.ds(pl.multiple_of(me * rows, rows), rows), :] = dot(feats_ref[...], rights[col]).astype(BF16)
     last = Gather(place, projs.at[col], rows, g_sends.at[2], g_recvs.at[2])
     last.open()
 
     chunk = 512
-    spread.wait()
 
     def gram_piece(lo, hi):
         def one(i, carry):
@@ -421,38 +491,56 @@
 
     gram_ref[...] = jnp.zeros_like(gram_ref)
     count = total_f // chunk
-    interleave(last.actions(), [functools.partial(gram_piece, i * count // 4, (i + 1) * count // 4) for i in range(4)])
-    last.close()
-    swap = Swap(place, projs.at[col], projs.at[col], s_sends, s_recvs, 2 * groups)
-    swaps.append(swap)
-
-    def lift(which):
+    steps = last.actions((m_sends, m_recvs, 0))
+    ready = min(place.lines, PLANE) - 1
+    mixed_ref[...] = jnp.zeros_like(mixed_ref)
+
+    def absorb(s):
+        block = beside([projs[t, last.line(s), :] for t in range(groups)])
+        mixed_ref[...] += dot(block, block, TN)
+
+    def lift(s, fresh):
         def one(i, carry):
             at = pl.ds(pl.multiple_of(i * chunk, chunk), chunk)
-            lifted_ref[which, at, :] = dot(lifts[at, :], projs[which]) * (1.0 / total_n)
+            left = lifts[at, last.line(s)]
+            for t in range(groups):
+                value = dot(left, projs[t, last.line(s), :]) * (1.0 / total_n)
+                lifted_ref[t, at, :] = value if fresh else lifted_ref[t, at, :] + value
             return carry
 
         lax.fori_loop(0, mine // chunk, one, 0)
 
-    lift(col)
-    swap.wait()
-    for other in place.others:
-        lift(other)
-
-    mixed_ref[...] = jnp.zeros_like(mixed_ref)
-
-    def mix(i, carry):
-        at = pl.ds(pl.multiple_of(i * chunk, chunk), chunk)
-        block = beside([projs[t, at, :] for t in range(groups)])
-        mixed_ref[...] += dot(block, block, TN)
-        return carry
-
-    lax.fori_loop(0, total_n // chunk, mix, 0)
+    grams = [functools.partial(gram_piece, i * count // 4, (i + 1) * count // 4) for i in range(4)]
+    interleave(steps[:-2], [*work[early:], spread.wait, *grams])
+    used = 0
+    for act in [*steps[-2:], lambda: None]:
+        if used < ready and used in last.mirrors:
+            last.mirrors[used].wait()
+            absorb(used)
+            lift(used, used == 0)
+            used += 1
+        act()
+    for s in range(used, place.lines):
+        last.mirrors[s].wait()
+    if place.lines - used <= PLANE:
+        for s in range(used, place.lines):
+            absorb(s)
+            lift(s, s == 0)
+    else:
+        def rest(s, carry):
+            absorb(s)
+            lift(s, False)
+            return carry
+
+        lax.fori_loop(used, place.lines, rest, 0)
     mixed_ref[...] = mixed_ref[...] * (1.0 / total_n) + ridge * gram_ref[...]
+
     own = pl.ds(pl.multiple_of(me * rows, rows), rows)
+    swaps[0].wait()
     for t in range(groups):
         part_ref[t] = rights[t, pl.ds(pl.multiple_of(col * mine, mine), mine), :]
         proj_ref[:, t * cols : (t + 1) * cols] = projs[t, own, :]
+        wide_ref[:, t * cols : (t + 1) * cols] = wides[t]
     for gather in (near, far, last):
         gather.drain()
     for swap in swaps:
@@ -475,19 +563,27 @@
             jax.ShapeDtypeStruct((groups, mine, cols), BF16),
             jax.ShapeDtypeStruct((rows, targets), BF16),
             jax.ShapeDtypeStruct((rows, total_f), BF16),
+            jax.ShapeDtypeStruct((feats, targets), F32),
         ],
-        in_specs=[VMEM] * 4,
-        out_specs=[VMEM] * 6,
+        in_specs=[pl.BlockSpec(memory_space=pltpu.HBM)] * 4,
+        out_specs=[VMEM] * 7,
         scratch_shapes=[
+            pltpu.VMEM((rows, depth), BF16),
+            pltpu.VMEM((depth, total_f), BF16),
+            pltpu.VMEM((1, total_f), F32),
+            pltpu.VMEM((groups, feats, cols), F32),
             pltpu.VMEM((pieces, total_n // pieces, depth), BF16),
             pltpu.VMEM((total_n, depth), BF16),
             pltpu.VMEM((groups, total_f, cols), BF16),
             pltpu.VMEM((groups, total_n, cols), BF16),
             pltpu.VMEM((mine, total_n), BF16),
+            pltpu.SemaphoreType.DMA((4,)),
             pltpu.SemaphoreType.DMA((3, slots(n))),
             pltpu.SemaphoreType.DMA((3, slots(n))),
             pltpu.SemaphoreType.DMA((3 * groups,)),
             pltpu.SemaphoreType.DMA((3 * groups,)),
+            pltpu.SemaphoreType.DMA((n // PLANE * groups,)),
+            pltpu.SemaphoreType.DMA((n // PLANE * groups,)),
         ],
         compiler_params=pltpu.CompilerParams(collective_id=0, has_side_effects=True, vmem_limit_bytes=room(groups)),
         cost_estimate=pl.CostEstimate(flops=10**11, bytes_accessed=2 * 2**20, transcendentals=0),
@@ -499,7 +595,7 @@
     n, groups, total_n,
     inverse_ref, gram_ref, lifted_ref, part_ref, proj_ref, feats_ref,
     first_ref, target_ref, final_ref, direction_ref,
-    resid, sums, theirs, aside, away, projs, shared, g_sends, g_recvs, s_sends, s_recvs,
+    resid, sums, theirs, aside, away, projs, shared, g_sends, g_recvs, s_sends, s_recvs, m_sends, m_recvs,
 ):
     place = Place(n, groups)
     me, col = place.me, place.col
@@ -507,7 +603,7 @@
     mine, cols = lifted_ref.shape[1:]
     targets = groups * cols
     chunk = 512
-    place.meet()
+    place.greet()
     inverse = halves(inverse_ref[...])
     alpha = dot_halves(inverse, halves(gram_ref[...]))
     alpha_halves = halves(alpha)
@@ -524,16 +620,15 @@
         resid[at, :] = left
         pair = halves(left)
         sums[0] += dot_halves(image, pair, TN)
-        sums[1] += dot_halves(pair, pair, TN)
         over = pl.ds(pl.multiple_of(col * mine + i * chunk, chunk), chunk)
         aside[...] += dot(feats_ref[:, over], pair[0])
         return carry
 
     lax.fori_loop(0, mine // chunk, one, 0)
+    place.meet()
     swaps = [
         Swap(place, sums.at[0], theirs.at[0], s_sends, s_recvs, 0, True),
         Swap(place, aside, away, s_sends, s_recvs, groups, True),
-        Swap(place, sums.at[1], theirs.at[1], s_sends, s_recvs, 2 * groups, True),
     ]
     swaps[0].wait()
 
@@ -562,21 +657,24 @@
     def turn(i):
         at = pl.ds(i * chunk, chunk)
         right = beside([part_ref[t, at, :] for t in range(groups)])
-        line = resid[at, :] + dot(right, beta_halves[0]) + dot(right, beta_halves[1])
+        left = resid[at, :]
+        pair = halves(left)
+        sums[1] += dot_halves(pair, pair, TN)
+        line = left + dot(right, beta_halves[0]) + dot(right, beta_halves[1])
         resid[at, :] = line
         pair = halves(line)
         final_ref[...] += dot_halves(pair, pair, TN)
 
-    interleave(gather.actions(), [functools.partial(turn, i) for i in range(mine // chunk)])
-    swaps[2].wait()
+    turns = [functools.partial(turn, i) for i in range(mine // chunk)]
+    steps = gather.actions((m_sends, m_recvs, 0))
+    cut = len(steps) * 2 // 3
+    interleave(steps[:cut], turns)
     swaps.append(Swap(place, final_ref, shared, s_sends, s_recvs, 3 * groups, True))
+    swaps.append(Swap(place, sums.at[1], theirs.at[1], s_sends, s_recvs, 2 * groups, True))
     feats = direction_ref.shape[0]
     owners = n // groups
     source = lax.div(me, owners)
     held = pl.ds(pl.multiple_of(lax.rem(me, owners) * feats, feats), feats)
-    new = total(1)
-    for t in range(groups):
-        pl.when(col == t)(functools.partial(target_ref.__setitem__, Ellipsis, new[:, t * cols : (t + 1) * cols]))
 
     def copies():
         return [
@@ -596,23 +694,40 @@
         for copy in copies():
             copy.start()
 
-    gather.close()
-    swaps.append(Swap(place, projs.at[col], projs.at[col], s_sends, s_recvs, 5 * groups))
-    swaps[3].wait()
-    swaps[3].drain()
+    steps[cut]()
+    swaps[2].wait()
+    swaps[2].drain()
     value = final_ref[...]
     for i in range(groups - 1):
         value = value + shared[i]
     final_ref[...] = ridge * value
-    swaps[4].wait()
-
-    def mix(i, carry):
-        at = pl.ds(pl.multiple_of(i * chunk, chunk), chunk)
-        block = beside([projs[t, at, :] for t in range(groups)])
+
+    def mix(s):
+        block = beside([projs[t, gather.line(s), :] for t in range(groups)])
         final_ref[...] += dot(block, block, TN) * (1.0 / total_n)
-        return carry
-
-    lax.fori_loop(0, total_n // chunk, mix, 0)
+
+    mixed = 0
+    for act in steps[cut + 1 :]:
+        act()
+        while mixed < min(place.lines, PLANE) - 2 and mixed in gather.mirrors:
+            gather.mirrors[mixed].wait()
+            mix(mixed)
+            mixed += 1
+    swaps[3].wait()
+    new = total(1)
+    for t in range(groups):
+        pl.when(col == t)(functools.partial(target_ref.__setitem__, Ellipsis, new[:, t * cols : (t + 1) * cols]))
+    for s in range(mixed, place.lines):
+        gather.mirrors[s].wait()
+    if place.lines - mixed <= PLANE:
+        for s in range(mixed, place.lines):
+            mix(s)
+    else:
+        def rest(s, carry):
+            mix(s)
+            return carry
+
+        lax.fori_loop(mixed, place.lines, rest, 0)
 
     @pl.when(col == source)
     def _():
@@ -626,7 +741,7 @@
         direction_ref[...] = resid[pl.ds(mine, feats), :]
 
     gather.drain()
-    for swap in swaps[:3] + swaps[4:]:
+    for swap in swaps[:2] + swaps[3:]:
         swap.drain()
 
 
@@ -655,8 +770,10 @@
             pltpu.VMEM((max(groups - 1, 1), targets, targets), F32),
             pltpu.SemaphoreType.DMA((slots(n),)),
             pltpu.SemaphoreType.DMA((slots(n),)),
-            pltpu.SemaphoreType.DMA((6 * groups,)),
-            pltpu.SemaphoreType.DMA((6 * groups,)),
+            pltpu.SemaphoreType.DMA((5 * groups,)),
+            pltpu.SemaphoreType.DMA((5 * groups,)),
+            pltpu.SemaphoreType.DMA((n // PLANE * groups,)),
+            pltpu.SemaphoreType.DMA((n // PLANE * groups,)),
         ],
         compiler_params=pltpu.CompilerParams(collective_id=1, has_side_effects=True, vmem_limit_bytes=room(groups)),
         cost_estimate=pl.CostEstimate(flops=10**11, bytes_accessed=2 * 2**20, transcendentals=0),
@@ -665,12 +782,11 @@
 
 
 def body(samples, omega, phase, right_side):
-    gram, mixed, lifted, part, proj, feats_own = first_stage(samples, omega, phase, right_side)
+    gram, mixed, lifted, part, proj, feats_own, right_all = first_stage(samples, omega, phase, right_side)
     inverse = inverse_of(mixed)
     first, target, final, direction = second_stage(
         inverse, gram, lifted, part, proj, feats_own, right_side.shape[0]
     )
-    right_all = lax.all_gather(right_side, "tgt", axis=1, tiled=True)
     return last_solve(final, target, right_all, first, direction)
 
 

time: 203 us -> 166 us (0.82)
  Pallas kernels: 197 us -> 161 us
  blocking collectives: 2.18 us -> 0 us
    pallas_call x1, Pallas kernels: 84.7 us -> 67.1 us  [first_stage(): pl.pallas_call(functools.partial(first_kernel, n, groups, total_n), out_s...]
    pallas_call x1, Pallas kernels: 34 us -> 26.7 us  [last_solve(): pl.pallas_call(last_kernel, out_shape=jax.ShapeDtypeStruct((direction.sha...]
    pallas_call x1, Pallas kernels: 31 us -> 24.5 us  [inverse_of(): pl.pallas_call(inverse_kernel, out_shape=jax.ShapeDtypeStruct((total, tot...]
    pallas_call x1, Pallas kernels: 47.1 us -> 42.2 us  [second_stage(): pl.pallas_call(functools.partial(second_kernel, n, groups, total_n), out_...]
    all_gather x1 -> x0, blocking collectives: 2.18 us -> none  [body(): right_all = lax.all_gather(right_side, 'tgt', axis=1, tiled=True)]
where the time goes in v2:
time: 166 us; the launch traced here: 164 us
  Pallas kernels  161 us (97%)
  local copies, waits for them, and re-layouts  3.69 us (2%)
    pallas_call x1, Pallas kernels, first_stage(): pl.pallas_call(functools.partial(first_kernel, n, groups, total_n), out_s...  67.1 us
    pallas_call x1, Pallas kernels, second_stage(): pl.pallas_call(functools.partial(second_kernel, n, groups, total_n), out_...  42.2 us
    pallas_call x1, Pallas kernels, last_solve(): pl.pallas_call(last_kernel, out_shape=jax.ShapeDtypeStruct((direction.sha...  26.7 us
    pallas_call x1, Pallas kernels, inverse_of(): pl.pallas_call(inverse_kernel, out_shape=jax.ShapeDtypeStruct((total, tot...  24.5 us
    unnamed x8, local copies, waits for them, and re-layouts  3.69 us

profile of v2, /device:TPU:1, one launch (start us, length us, event | category | flops | bytes accessed | tf_op | source)
XLA Modules:
  0.0 164.3 jit_solution(12242932237345712860)
XLA Ops:
  0.0 0.0 copy-start
  0.0 1.2 copy-done
  1.2 0.0 copy-start.1
  1.2 0.9 copy-done.1
  2.2 0.0 copy-start.2
  2.2 0.8 copy-done.2
  3.0 0.0 copy-start.3
  3.0 0.7 copy-done.3
  3.7 67.1 %first.1 = (f32[512,512]{1,0:T(8,128)S(1)}, f32[512,512]{1,0:T(8,128)S(1)}, f32[2,2048,256]{2,1,0:T(8,128)S(1)}, bf16[2,2048,256]{2,1,0:T(8,128)(2,1)S(1)}, bf16...) custom-call(bf16[192,128]{1,0:T(8,128)(2,1)S(1)} %copy-done.2, ...), custom_call_target="tpu_custom_call" | custom-call | flops 99999997952 | bytes 2097152 | tf_op jit(solution)/shard_map/first/pallas_call | solution.py:557
  70.8 24.5 %inverse.1.inverse_ref = f32[512,512]{1,0:T(8,128)S(1)} custom-call(f32[512,512]{1,0:T(8,128)S(1)} %get-tuple-element.16.gram_ref), custom_call_target="tpu_custom_call" | custom-call | flops 20000000000 | bytes 2097152 | tf_op jit(solution)/shard_map/inverse/pallas_call | solution.py:157
  95.3 42.2 %second.1 = (f32[512,256]{1,0:T(8,128)S(1)}, f32[512,256]{1,0:T(8,128)S(1)}, f32[512,512]{1,0:T(8,128)S(1)}, f32[256,512]{1,0:T(8,128)S(1)}) custom-call(f32[512,512]{1,0:T(8,128)S(1)} %inverse.1.inverse_ref, f32[512,512]{1,0:T(8,128)S(1)} %get-tuple-element.17.gram_ref, f32[2,2048,256]{2,1,0:T(8,128)S(1)} %get-tuple-element.18.lifted_ref, ...), custom_call_target="tpu_custom_call" | custom-call | flops 99999997952 | bytes 2097152 | tf_op jit(solution)/shard_map/second/pallas_call | solution.py:753
  137.6 26.7 %last.1 = f32[256,256]{1,0:T(8,128)} custom-call(f32[512,512]{1,0:T(8,128)S(1)} %get-tuple-element.22.gram_ref, f32[512,256]{1,0:T(8,128)S(1)} %get-tuple-element.23.rhs_ref, f32[256,512]{1,0:T(8,128)S(1)} %get-tuple-element.24.right_ref, f32[512,256]{1,0:T(8,128)S(1)} %get-tuple-element.25.first_ref, f32[256,512]{1,0:T(8,128)S(1)} %get-tuple-element.26.direction_ref), custom_call_target="tpu_custom_call" | custom-call | flops 20000000000 | bytes 3145728 | tf_op jit(solution)/shard_map/last/pallas_call | solution.py:207
Async XLA Ops:
  0.0 1.2 copy-start
  1.2 0.9 copy-start.1
  2.2 0.8 copy-start.2
  3.0 0.7 copy-start.3

commit v3 on v2

--- a/solution.py
+++ b/solution.py
@@ -77,7 +77,7 @@
     return [[-at(i, j) for j in range(size)] for i in range(size)]
 
 
-def invert_block(value):
+def invert_block(value, unit):
     size = value.shape[0]
     tiles = [value[t * 8 : t * 8 + 8, :] for t in range(size // 8)]
     lane = lax.broadcasted_iota(jnp.int32, (8, size), 1)
@@ -86,7 +86,7 @@
         j = g * GROUP
         in_group = (lane >= j) & (lane < j + GROUP)
         home = tiles[g]
-        spread = [jnp.broadcast_to(home[:, j + m : j + m + 1], (8, size)) for m in range(GROUP)]
+        spread = [jnp.broadcast_to(home[:, j + m : j + m + 1], (8, size)) * unit for m in range(GROUP)]
         rows = [
             jnp.where(in_group, jnp.where(lane == j + k, 1.0, 0.0), jnp.broadcast_to(home[k : k + 1, :], (8, size)))
             for k in range(GROUP)
@@ -116,7 +116,7 @@
     return jnp.concatenate(tiles, axis=0)
 
 
-def inverse_kernel(gram_ref, work, row, column):
+def inverse_kernel(gram_ref, work, row, column, ones):
     total = gram_ref.shape[0]
     size = BLOCK
     count = total // size
@@ -124,10 +124,11 @@
     work[...] = gram_ref[...] * scale
     row[...] = jnp.zeros_like(row)
     column[...] = jnp.zeros_like(column)
+    ones[...] = jnp.ones_like(ones)
 
     def step(k, carry):
         at = pl.ds(pl.multiple_of(k * size, size), size)
-        inv = invert_block(work[at, at])
+        inv = invert_block(work[at, at], ones[...])
         for i in range(1, count):
             rows = pl.ds(pl.multiple_of(lax.rem(k + i, count) * size, size), size)
             work[rows, :] = work[rows, :] - precise_dot(column[rows, :], row[...])
@@ -159,14 +160,18 @@
         out_shape=jax.ShapeDtypeStruct((total, total), F32),
         in_specs=[VMEM],
         out_specs=VMEM,
-        scratch_shapes=[pltpu.VMEM((BLOCK, total), F32), pltpu.VMEM((total, BLOCK), F32)],
+        scratch_shapes=[
+            pltpu.VMEM((BLOCK, total), F32),
+            pltpu.VMEM((total, BLOCK), F32),
+            pltpu.VMEM((8, BLOCK), F32),
+        ],
         compiler_params=pltpu.CompilerParams(vmem_limit_bytes=16 * 2**20),
         cost_estimate=pl.CostEstimate(flops=2 * 10**10, bytes_accessed=2 * 2**20, transcendentals=0),
         name="inverse",
     )(gram)
 
 
-def last_kernel(gram_ref, rhs_ref, right_ref, first_ref, direction_ref, out_ref, work, row, column):
+def last_kernel(gram_ref, rhs_ref, right_ref, first_ref, direction_ref, out_ref, work, row, column, ones):
     total, cols = rhs_ref.shape
     size = BLOCK
     count = total // size
@@ -175,11 +180,12 @@
     work[:, total:] = rhs_ref[...] * scale
     row[...] = jnp.zeros_like(row)
     column[...] = jnp.zeros_like(column)
+    ones[...] = jnp.ones_like(ones)
     out_ref[...] = dot_halves(halves(right_ref[...]), halves(first_ref[...]))
 
     def step(k, carry):
         at = pl.ds(pl.multiple_of(k * size, size), size)
-        inv = invert_block(work[at, at])
+        inv = invert_block(work[at, at], ones[...])
         for i in range(1, count):
             rows = pl.ds(pl.multiple_of(lax.rem(k + i, count) * size, size), size)
             work[rows, :] = work[rows, :] - precise_dot(column[rows, :], row[...])
@@ -213,6 +219,7 @@
             pltpu.VMEM((total, total + cols), F32),
             pltpu.VMEM((BLOCK, total + cols), F32),
             pltpu.VMEM((total, BLOCK), F32),
+            pltpu.VMEM((8, BLOCK), F32),
         ],
         compiler_params=pltpu.CompilerParams(vmem_limit_bytes=24 * 2**20),
         cost_estimate=pl.CostEstimate(flops=2 * 10**10, bytes_accessed=3 * 2**20, transcendentals=0),
@@ -314,16 +321,17 @@
             self.mirrors[s] = Swap(self.place, ref, ref, sends, recvs, base + s * self.place.groups)
 
     def actions(self, mirror=None):
-        steps, lines = [], self.place.lines
+        lines = self.place.lines
+        steps = [functools.partial(self.corner, 0)]
+        steps += [functools.partial(self.relay, s) for s in range(1, min(lines, 4))]
         for s in range(1, lines):
-            steps.append(functools.partial(self.relay, s))
-            steps.append(functools.partial(self.corner, s - 1))
-            if mirror is not None and s > 1:
-                steps.append(functools.partial(self.finish, s - 2, mirror))
-        steps.append(functools.partial(self.corner, lines - 1))
+            steps.append(functools.partial(self.corner, s))
+            if s + 3 < lines:
+                steps.append(functools.partial(self.relay, s + 3))
+            if mirror is not None:
+                steps.append(functools.partial(self.finish, s - 1, mirror))
         if mirror is not None:
-            for s in range(max(lines - 2, 0), lines):
-                steps.append(functools.partial(self.finish, s, mirror))
+            steps.append(functools.partial(self.finish, lines - 1, mirror))
         return steps
 
     def close(self):
@@ -588,7 +596,7 @@
         compiler_params=pltpu.CompilerParams(collective_id=0, has_side_effects=True, vmem_limit_bytes=room(groups)),
         cost_estimate=pl.CostEstimate(flops=10**11, bytes_accessed=2 * 2**20, transcendentals=0),
         name="first",
-    )(samples, omega, phase.reshape(1, -1), right_side)
+    )(*[pltpu.with_memory_space_constraint(x, pltpu.HBM) for x in (samples, omega, phase.reshape(1, -1), right_side)])
 
 
 def second_kernel(
@@ -695,16 +703,12 @@
             copy.start()
 
     steps[cut]()
-    swaps[2].wait()
-    swaps[2].drain()
-    value = final_ref[...]
-    for i in range(groups - 1):
-        value = value + shared[i]
-    final_ref[...] = ridge * value
+    swaps[0].drain()
+    sums[0] = jnp.zeros((targets, targets), F32)
 
     def mix(s):
         block = beside([projs[t, gather.line(s), :] for t in range(groups)])
-        final_ref[...] += dot(block, block, TN) * (1.0 / total_n)
+        sums[0] += dot(block, block, TN)
 
     mixed = 0
     for act in steps[cut + 1 :]:
@@ -729,6 +733,13 @@
 
         lax.fori_loop(mixed, place.lines, rest, 0)
 
+    swaps[2].wait()
+    swaps[2].drain()
+    value = final_ref[...]
+    for i in range(groups - 1):
+        value = value + shared[i]
+    final_ref[...] = ridge * value + sums[0] * (1.0 / total_n)
+
     @pl.when(col == source)
     def _():
         direction_ref[...] = resid[held, :]
@@ -741,7 +752,7 @@
         direction_ref[...] = resid[pl.ds(mine, feats), :]
 
     gather.drain()
-    for swap in swaps[:2] + swaps[3:]:
+    for swap in [swaps[1], swaps[3]]:
         swap.drain()
 
 

time: 166 us -> 157 us (0.946); the launches traced: 164 us -> 157 us
  Pallas kernels: 161 us -> 157 us
  local copies, waits for them, and re-layouts: 3.69 us -> 0 us
    unnamed x8 -> x0, local copies, waits for them, and re-layouts: 3.69 us -> none
where the time goes in v3:
time: 157 us
  Pallas kernels  157 us (100%)
    pallas_call x1, Pallas kernels, first_stage(): pl.pallas_call(functools.partial(first_kernel, n, groups, total_n), out_s...  65.6 us
    pallas_call x1, Pallas kernels, second_stage(): pl.pallas_call(functools.partial(second_kernel, n, groups, total_n), out_...  42.1 us
    pallas_call x1, Pallas kernels, last_solve(): pl.pallas_call(last_kernel, out_shape=jax.ShapeDtypeStruct((direction.sha...  25.4 us
    pallas_call x1, Pallas kernels, inverse_of(): pl.pallas_call(inverse_kernel, out_shape=jax.ShapeDtypeStruct((total, tot...  23.8 us

profile of v3, /device:TPU:1, one launch (start us, length us, event | category | flops | bytes accessed | tf_op | source)
XLA Modules:
  0.0 157.0 jit_solution(9862755213899518116)
XLA Ops:
  0.0 65.6 %first.1 = (f32[512,512]{1,0:T(8,128)S(1)}, f32[512,512]{1,0:T(8,128)S(1)}, f32[2,2048,256]{2,1,0:T(8,128)S(1)}, bf16[2,2048,256]{2,1,0:T(8,128)(2,1)S(1)}, bf16...) custom-call(bf16[192,128]{1,0:T(8,128)(2,1)} %samples_hbm.1, ...), custom_call_target="tpu_custom_call" | custom-call | flops 99999997952 | bytes 2097152 | tf_op jit(solution)/shard_map/first/pallas_call | solution.py:565
  65.7 23.8 %inverse.1.inverse_ref = f32[512,512]{1,0:T(8,128)S(1)} custom-call(f32[512,512]{1,0:T(8,128)S(1)} %get-tuple-element.16.gram_ref), custom_call_target="tpu_custom_call" | custom-call | flops 20000000000 | bytes 2097152 | tf_op jit(solution)/shard_map/inverse/pallas_call | solution.py:158
  89.4 42.1 %second.1 = (f32[512,256]{1,0:T(8,128)S(1)}, f32[512,256]{1,0:T(8,128)S(1)}, f32[512,512]{1,0:T(8,128)S(1)}, f32[256,512]{1,0:T(8,128)S(1)}) custom-call(f32[512,512]{1,0:T(8,128)S(1)} %inverse.1.inverse_ref, f32[512,512]{1,0:T(8,128)S(1)} %get-tuple-element.17.gram_ref, f32[2,2048,256]{2,1,0:T(8,128)S(1)} %get-tuple-element.18.lifted_ref, ...), custom_call_target="tpu_custom_call" | custom-call | flops 99999997952 | bytes 2097152 | tf_op jit(solution)/shard_map/second/pallas_call | solution.py:764
  131.6 25.4 %last.1 = f32[256,256]{1,0:T(8,128)} custom-call(f32[512,512]{1,0:T(8,128)S(1)} %get-tuple-element.22.gram_ref, f32[512,256]{1,0:T(8,128)S(1)} %get-tuple-element.23.rhs_ref, f32[256,512]{1,0:T(8,128)S(1)} %get-tuple-element.24.right_ref, f32[512,256]{1,0:T(8,128)S(1)} %get-tuple-element.25.first_ref, f32[256,512]{1,0:T(8,128)S(1)} %get-tuple-element.26.direction_ref), custom_call_target="tpu_custom_call" | custom-call | flops 20000000000 | bytes 3145728 | tf_op jit(solution)/shard_map/last/pallas_call | solution.py:213

commit v4 on v3

--- a/solution.py
+++ b/solution.py
@@ -519,7 +519,7 @@
         lax.fori_loop(0, mine // chunk, one, 0)
 
     grams = [functools.partial(gram_piece, i * count // 4, (i + 1) * count // 4) for i in range(4)]
-    interleave(steps[:-2], [*work[early:], spread.wait, *grams])
+    interleave(steps[:-2], [*work[early : early + 1], spread.wait, *grams, *work[early + 1 :]])
     used = 0
     for act in [*steps[-2:], lambda: None]:
         if used < ready and used in last.mirrors:

time: 157 us -> 158 us (level)
    pallas_call x1, Pallas kernels: 65.6 us -> 67.4 us  [first_stage(): pl.pallas_call(functools.partial(first_kernel, n, groups, total_n), out_s...]
where the time goes in v4:
time: 158 us; the launch traced here: 157 us
  Pallas kernels  157 us (99%)
    pallas_call x1, Pallas kernels, first_stage(): pl.pallas_call(functools.partial(first_kernel, n, groups, total_n), out_s...  67.4 us
    pallas_call x1, Pallas kernels, second_stage(): pl.pallas_call(functools.partial(second_kernel, n, groups, total_n), out_...  40.7 us
    pallas_call x1, Pallas kernels, last_solve(): pl.pallas_call(last_kernel, out_shape=jax.ShapeDtypeStruct((direction.sha...  25.4 us
    pallas_call x1, Pallas kernels, inverse_of(): pl.pallas_call(inverse_kernel, out_shape=jax.ShapeDtypeStruct((total, tot...  23.8 us

profile of v4, /device:TPU:1, one launch (start us, length us, event | category | flops | bytes accessed | tf_op | source)
XLA Modules:
  0.0 157.3 jit_solution(13184541439194097761)
XLA Ops:
  0.0 67.4 %first.1 = (f32[512,512]{1,0:T(8,128)S(1)}, f32[512,512]{1,0:T(8,128)S(1)}, f32[2,2048,256]{2,1,0:T(8,128)S(1)}, bf16[2,2048,256]{2,1,0:T(8,128)(2,1)S(1)}, bf16...) custom-call(bf16[192,128]{1,0:T(8,128)(2,1)} %samples_hbm.1, ...), custom_call_target="tpu_custom_call" | custom-call | flops 99999997952 | bytes 2097152 | tf_op jit(solution)/shard_map/first/pallas_call | solution.py:565
  67.4 23.8 %inverse.1.inverse_ref = f32[512,512]{1,0:T(8,128)S(1)} custom-call(f32[512,512]{1,0:T(8,128)S(1)} %get-tuple-element.16.gram_ref), custom_call_target="tpu_custom_call" | custom-call | flops 20000000000 | bytes 2097152 | tf_op jit(solution)/shard_map/inverse/pallas_call | solution.py:158
  91.2 40.7 %second.1 = (f32[512,256]{1,0:T(8,128)S(1)}, f32[512,256]{1,0:T(8,128)S(1)}, f32[512,512]{1,0:T(8,128)S(1)}, f32[256,512]{1,0:T(8,128)S(1)}) custom-call(f32[512,512]{1,0:T(8,128)S(1)} %inverse.1.inverse_ref, f32[512,512]{1,0:T(8,128)S(1)} %get-tuple-element.17.gram_ref, f32[2,2048,256]{2,1,0:T(8,128)S(1)} %get-tuple-element.18.lifted_ref, ...), custom_call_target="tpu_custom_call" | custom-call | flops 99999997952 | bytes 2097152 | tf_op jit(solution)/shard_map/second/pallas_call | solution.py:764
  131.9 25.4 %last.1 = f32[256,256]{1,0:T(8,128)} custom-call(f32[512,512]{1,0:T(8,128)S(1)} %get-tuple-element.22.gram_ref, f32[512,256]{1,0:T(8,128)S(1)} %get-tuple-element.23.rhs_ref, f32[256,512]{1,0:T(8,128)S(1)} %get-tuple-element.24.right_ref, f32[512,256]{1,0:T(8,128)S(1)} %get-tuple-element.25.first_ref, f32[256,512]{1,0:T(8,128)S(1)} %get-tuple-element.26.direction_ref), custom_call_target="tpu_custom_call" | custom-call | flops 20000000000 | bytes 3145728 | tf_op jit(solution)/shard_map/last/pallas_call | solution.py:213
